TPU v7x, 8 devices: a whole 2x2x1 slice. The times are simulated.
8 devices in a mesh: dp: 1 (over z), tp: 2 (over y), cp: 4 (over x, core).
Axes of the slice: x: 2, y: 2, z: 1, core: 2. Of those that a mesh axis runs over, the one named last changes fastest.
Arguments:
- hidden: bfloat16 [8192, 2304], P(('dp', 'cp'))
- positions: int32 [8192], P(('dp', 'cp'))
- w_q: bfloat16 [2, 2304, 2048], P(None, None, 'tp')
- w_k: bfloat16 [2, 2304, 1024], P(None, None, 'tp')
- w_v: bfloat16 [2, 2304, 1024], P(None, None, 'tp')
- w_o: bfloat16 [2, 2048, 2304], P(None, 'tp')
- w_gate: bfloat16 [2, 2304, 9216], P(None, None, 'tp')
- w_up: bfloat16 [2, 2304, 9216], P(None, None, 'tp')
- w_down: bfloat16 [2, 9216, 2304], P(None, 'tp')
- norm_gain: float32 [2, 4, 2304], replicated
- qk_gain: float32 [2, 2, 256], replicated
Outputs:
- output 1: bfloat16 [8192, 2304], P(('dp', 'cp'))
- output 2: bfloat16 [2, 8192, 4, 256], P(None, ('dp', 'cp'), 'tp')
- output 3: bfloat16 [2, 8192, 4, 256], P(None, ('dp', 'cp'), 'tp')
All inputs are finite; a program needn't handle non-finite values.
Results may differ from a plain program's by a relative error of at most 0.0163912.
Values are sent between devices in bfloat16 or wider.
A program may use at most 1 GiB of HBM per device.

v0:
```python
import math
import jax
import jax.numpy as jnp
from jax import lax
from jax.sharding import PartitionSpec as P

WINDOW = 1024
THETAS = (10000.0, 1000000.0)
EPS = 1e-6
NEG_BIG = -1e30


def rms_scale(values, gain):
    mean_sq = jnp.mean(values * values, axis=-1, keepdims=True)
    return values * lax.rsqrt(mean_sq + EPS) * (1.0 + gain)


def rotary(values, positions, theta):
    head_dim = values.shape[-1]
    half_dim = head_dim // 2
    inv_freq = theta ** (-(jnp.arange(half_dim, dtype=jnp.float32) * 2.0) / head_dim)
    angles = positions.astype(jnp.float32)[..., None] * inv_freq
    cosine = jnp.cos(angles)[..., None, :]
    sine_val = jnp.sin(angles)[..., None, :]
    lower_half = values[..., :half_dim]
    upper_half = values[..., half_dim:]
    return jnp.concatenate([lower_half * cosine - upper_half * sine_val, upper_half * cosine + lower_half * sine_val], axis=-1)


def project_qkv(state_f, positions, w_q, w_k, w_v, layer_gain, qk_pair, theta, head_dim):
    normed = rms_scale(state_f, layer_gain[0]).astype(jnp.bfloat16)
    head_shape = normed.shape[:-1] + (-1, head_dim)
    q_proj = jnp.dot(normed, w_q, preferred_element_type=jnp.float32).reshape(head_shape)
    k_proj = jnp.dot(normed, w_k, preferred_element_type=jnp.float32).reshape(head_shape)
    v_rows = jnp.dot(normed, w_v, preferred_element_type=jnp.float32).astype(jnp.bfloat16).reshape(head_shape)
    q_rot = rotary(rms_scale(q_proj, qk_pair[0]), positions, theta).astype(jnp.bfloat16)
    k_rot = rotary(rms_scale(k_proj, qk_pair[1]), positions, theta).astype(jnp.bfloat16)
    return q_rot, k_rot, v_rows


def attend(queries, key_rows, val_rows, q_start, k_start, window, lo_block, hi_block, block_len):
    n_query, kv_local, groups, head_dim = queries.shape
    score_scale = head_dim ** -0.5
    query_index = q_start + jnp.arange(n_query)
    init_state = (
        jnp.full((kv_local, groups, n_query, 1), NEG_BIG, jnp.float32),
        jnp.zeros((kv_local, groups, n_query, 1), jnp.float32),
        jnp.zeros((kv_local, groups, n_query, head_dim), jnp.float32),
    )

    def loop_body(step_id, loop_state):
        run_max, run_sum, acc_out = loop_state
        key_blk = lax.dynamic_slice_in_dim(key_rows, step_id * block_len, block_len, 0)
        val_blk = lax.dynamic_slice_in_dim(val_rows, step_id * block_len, block_len, 0)
        scores = jnp.einsum('qhgd,uhd->hgqu', queries, key_blk, preferred_element_type=jnp.float32) * score_scale
        key_index = k_start + step_id * block_len + jnp.arange(block_len)
        distance = query_index[:, None] - key_index[None, :]
        allowed = (distance >= 0) & (distance < window) & (key_index >= 0)[None, :]
        scores = jnp.where(allowed, scores, NEG_BIG)
        new_max = jnp.maximum(run_max, jnp.max(scores, axis=-1, keepdims=True))
        prob_blk = jnp.exp(scores - new_max)
        factor = jnp.exp(run_max - new_max)
        run_sum = run_sum * factor + jnp.sum(prob_blk, axis=-1, keepdims=True)
        acc_out = acc_out * factor + jnp.einsum('hgqu,uhd->hgqd', prob_blk.astype(jnp.bfloat16), val_blk, preferred_element_type=jnp.float32)
        return new_max, run_sum, acc_out

    run_max, run_sum, acc_out = lax.fori_loop(lo_block, hi_block, loop_body, init_state)
    result = (acc_out / run_sum).astype(jnp.bfloat16)
    return jnp.transpose(result, (2, 0, 1, 3)).reshape(n_query, kv_local * groups * head_dim)


def finish_layer(state_f, attn_rows, w_o, w_gate, w_up, w_down, layer_gain):
    attn_out = lax.psum(jnp.dot(attn_rows, w_o, preferred_element_type=jnp.float32), 'tp')
    resid_f = (state_f + rms_scale(attn_out, layer_gain[1])).astype(jnp.bfloat16).astype(jnp.float32)
    normed = rms_scale(resid_f, layer_gain[2]).astype(jnp.bfloat16)
    gate_proj = jnp.dot(normed, w_gate, preferred_element_type=jnp.float32)
    up_proj = jnp.dot(normed, w_up, preferred_element_type=jnp.float32)
    act_rows = (jax.nn.gelu(gate_proj, approximate=True) * up_proj).astype(jnp.bfloat16)
    mlp_out = lax.psum(jnp.dot(act_rows, w_down, preferred_element_type=jnp.float32), 'tp')
    return (resid_f + rms_scale(mlp_out, layer_gain[3])).astype(jnp.bfloat16)


def solution(mesh):
    cp_size = mesh.shape['cp']
    row_spec = P(('dp', 'cp'), None)
    col_spec = P(None, None, 'tp')
    row_w_spec = P(None, 'tp', None)
    cache_spec = P(None, ('dp', 'cp'), 'tp', None)

    def device_fn(hidden, positions, w_q, w_k, w_v, w_o, w_gate, w_up, w_down, norm_gain, qk_gain):
        tok_rows = hidden.shape[0]
        head_dim = qk_gain.shape[-1]
        kv_local = w_k.shape[-1] // head_dim
        groups = w_q.shape[-1] // w_k.shape[-1]
        block_len = math.gcd(tok_rows, 256)
        q_start = lax.axis_index('cp') * tok_rows
        hi_block = (q_start + tok_rows) // block_len
        state_f = hidden.astype(jnp.float32)
        new_hidden = hidden
        k_list = []
        v_list = []
        for layer_id in range(2):
            q_rot, k_rot, v_rows = project_qkv(state_f, positions, w_q[layer_id], w_k[layer_id], w_v[layer_id], norm_gain[layer_id], qk_gain[layer_id], THETAS[layer_id], head_dim)
            k_all = lax.all_gather(k_rot, 'cp', axis=0, tiled=True)
            v_all = lax.all_gather(v_rows, 'cp', axis=0, tiled=True)
            if layer_id == 0:
                window = WINDOW
                lo_block = jnp.maximum(q_start - (WINDOW - 1), 0) // block_len
            else:
                window = tok_rows * cp_size
                lo_block = jnp.zeros((), jnp.int32)
            q_group = q_rot.reshape(tok_rows, kv_local, groups, head_dim)
            attn_rows = attend(q_group, k_all, v_all, q_start, 0, window, lo_block, hi_block, block_len)
            new_hidden = finish_layer(state_f, attn_rows, w_o[layer_id], w_gate[layer_id], w_up[layer_id], w_down[layer_id], norm_gain[layer_id])
            state_f = new_hidden.astype(jnp.float32)
            k_list.append(k_rot)
            v_list.append(v_rows)
        return new_hidden, jnp.stack(k_list), jnp.stack(v_list)

    return jax.shard_map(
        device_fn,
        mesh=mesh,
        in_specs=(row_spec, P(('dp', 'cp')), col_spec, col_spec, col_spec, row_w_spec, col_spec, col_spec, row_w_spec, P(), P()),
        out_specs=(row_spec, cache_spec, cache_spec),
        check_vma=False,
    )
```

profile of v0, /device:TPU:0, one launch (start us, length us, event | category | flops | bytes accessed | tf_op | source)
XLA Modules:
  0.0 3089.4 jit_solution(15746363530761916)
XLA Ops:
  70.8 14.1 multiply_reduce_fusion.5
  100.8 56.7 %all-gather.7.cloned.1.call-done = bf16[8192,2,256]{2,0,1:T(8,128)(2,1)} async-done(((bf16[2048,2,256]{2,0,1:T(8,128)(2,1)}), bf16[8192,2,256]{2,0,1:T(8,128)(2,1)}) %all-gather.7.cloned.1.call-update) | async-done | bytes 8388624 | tf_op jit(solution)/shard_map/all_gather | solution.py:105
  161.7 115.6 %while.30 = (s32[]{:T(128)}, f32[2,2,2048,1]{2,1,0,3:T(2,128)S(1)}, f32[2,2,2048,1]{2,1,0,3:T(2,128)S(1)}, f32[2,2,2048,256]{3,2,1,0:T(8,128)}, s32[]{:T(128)}, ...) while((s32[]{:T(128)}, f32[2,2,2048,1]{2,1,0,3:T(2,128)S(1)}, ...), condition=%wide.region_6.7_spmd.clone, body=%wide.region_3.6_spmd.clone.sunk | while | flops 2177395456 | bytes 116411128 | solution.py:67
  290.6 15.4 fusion.104
  306.3 474.8 %all-reduce.5.cloned.1.call-done = f32[2048,2304]{1,0:T(8,128)} async-done(((f32[2048,2304]{1,0:T(8,128)}), f32[2048,2304]{1,0:T(8,128)}) %all-reduce.5.cloned.1.call-update) | async-done | bytes 18874384 | tf_op jit(solution)/shard_map/psum | solution.py:73
  788.7 10.8 fusion.82
  803.3 51.0 %fusion.70 = f32[2048,4608]{1,0:T(8,128)} fusion(bf16[2,2304,4608]{2,1,0:T(8,128)(2,1)} %param.21, bf16[2048,2304]{1,0:T(8,128)(2,1)S(1)} %get-tuple-element.244, f32[2304]{0:T(1024)S(1)} %copy-done.24, f32[2048]{0:T(1024)S(1)} %add_rsqrt_fusion.9), kind=kOutput, calls=%fused_computation.102 | convolution fusion | flops 43505418240 | bytes 68436992 | tf_op jit(solution)/shard_map/dot_general | solution.py:76
  854.3 64.9 %fusion.52 = bf16[2048,4608]{1,0:T(8,128)(2,1)} fusion(f32[2048,4608]{1,0:T(8,128)} %fusion.70, bf16[2,2304,4608]{2,1,0:T(8,128)(2,1)} %param.22, bf16[2048,2304]{1,0:T(8,128)(2,1)} %copy-done.5, f32[2304]{0:T(1024)S(1)} %copy-done.24, f32[2048]{0:T(1024)S(1)} %add_rsqrt_fusion.9), kind=kOutput, calls=%fused_computation.72 | convolution fusion | flops 43599790080 | bytes 87311360 | tf_op jit(solution)/shard_map/dot_general | solution.py:77
  919.1 56.6 %fusion.67 = f32[2048,2304]{1,0:T(8,128)} fusion(bf16[2048,4608]{1,0:T(8,128)(2,1)} %fusion.52, bf16[2,4608,2304]{2,1,0:T(8,128)(2,1)} %param.23), kind=kOutput, calls=%fused_computation.99 | convolution fusion | flops 43486543872 | bytes 58982400 | tf_op jit(solution)/shard_map/dot_general | solution.py:79
  975.9 418.4 %all-reduce.7.cloned.1.call-done = f32[2048,2304]{1,0:T(8,128)} async-done(((f32[2048,2304]{1,0:T(8,128)}), f32[2048,2304]{1,0:T(8,128)}) %all-reduce.7.cloned.1.call-update) | async-done | bytes 18874384 | tf_op jit(solution)/shard_map/psum | solution.py:79
  1401.9 10.8 fusion.86
  1412.8 10.2 convolution_convert_fusion
  1450.5 14.1 multiply_reduce_fusion.4
  1483.9 57.7 %all-gather.9.cloned.1.call-done = bf16[8192,2,256]{0,2,1:T(8,128)(2,1)} async-done(((bf16[2048,2,256]{0,2,1:T(8,128)(2,1)}), bf16[8192,2,256]{0,2,1:T(8,128)(2,1)}) %all-gather.9.cloned.1.call-update) | async-done | bytes 8388624 | tf_op jit(solution)/shard_map/all_gather | solution.py:104
  1545.5 113.8 %while.31 = (s32[]{:T(128)}, f32[2,2,2048,1]{2,1,0,3:T(2,128)S(1)}, f32[2,2,2048,1]{2,1,0,3:T(2,128)S(1)}, f32[2,2,2048,256]{3,2,1,0:T(8,128)}, s32[]{:T(128)}, ...) while((s32[]{:T(128)}, f32[2,2,2048,1]{2,1,0,3:T(2,128)S(1)}, ...), condition=%wide.region_18.19_spmd.clone, body=%wide.region_15.18_spmd.clone.sunk | while | flops 2177395456 | bytes 116411128 | solution.py:67
  1672.6 15.4 fusion.102
  1688.3 758.3 %all-reduce.9.cloned.1.call-done = f32[2048,2304]{1,0:T(8,128)} async-done(((f32[2048,2304]{1,0:T(8,128)}), f32[2048,2304]{1,0:T(8,128)}) %all-reduce.9.cloned.1.call-update) | async-done | bytes 18874384 | tf_op jit(solution)/shard_map/psum | solution.py:73
  2454.3 10.8 fusion.90
  2468.8 51.0 %fusion.65 = f32[2048,4608]{1,0:T(8,128)} fusion(bf16[2,2304,4608]{2,1,0:T(8,128)(2,1)} %param.21, bf16[2048,2304]{1,0:T(8,128)(2,1)S(1)} %get-tuple-element.240, f32[2304]{0:T(1024)S(1)} %copy-done.22, f32[2048]{0:T(1024)S(1)} %add_rsqrt_fusion.5), kind=kOutput, calls=%fused_computation.97 | convolution fusion | flops 43505418240 | bytes 68436992 | tf_op jit(solution)/shard_map/dot_general | solution.py:76
  2519.8 64.9 %fusion.61 = bf16[2048,4608]{1,0:T(8,128)(2,1)} fusion(f32[2048,4608]{1,0:T(8,128)} %fusion.65, bf16[2,2304,4608]{2,1,0:T(8,128)(2,1)} %param.22, bf16[2048,2304]{1,0:T(8,128)(2,1)} %copy-done.6, f32[2304]{0:T(1024)S(1)} %copy-done.22, f32[2048]{0:T(1024)S(1)} %add_rsqrt_fusion.5), kind=kOutput, calls=%fused_computation.81 | convolution fusion | flops 43599790080 | bytes 87311360 | tf_op jit(solution)/shard_map/dot_general | solution.py:77
  2584.7 56.7 %fusion.62 = f32[2048,2304]{1,0:T(8,128)} fusion(bf16[2048,4608]{1,0:T(8,128)(2,1)} %fusion.61, bf16[2,4608,2304]{2,1,0:T(8,128)(2,1)} %param.23), kind=kOutput, calls=%fused_computation.94 | convolution fusion | flops 43486543872 | bytes 58982400 | tf_op jit(solution)/shard_map/dot_general | solution.py:79
  2651.0 11.3 copy.49
  2675.6 384.3 %all-reduce.11.cloned.1.call-done = f32[2048,2304]{1,0:T(8,128)} async-done(((f32[2048,2304]{1,0:T(8,128)}), f32[2048,2304]{1,0:T(8,128)}) %all-reduce.11.cloned.1.call-update) | async-done | bytes 18874384 | tf_op jit(solution)/shard_map/psum | solution.py:79
  3067.5 14.5 fusion.93
  (360 shorter events, 449.5 us)
Async XLA Ops:
  7.2 93.7 %all-gather.5.cloned.1.call-start = ((), (), s32[]{:S(2)}) async-start(), calls=%async_computation | async-start | bytes 10485760 | tf_op jit(solution)/shard_map/all_gather | solution.py:104
  7.2 7.6 slice-start
  19.0 8.7 copy-start.28
  19.0 9.3 copy-start.25
  41.6 116.0 %all-gather.7.cloned.1.call-start = ((), (), s32[]{:S(2)}) async-start(), calls=%async_computation.1 | async-start | bytes 10485760 | tf_op jit(solution)/shard_map/all_gather | solution.py:105
  55.3 725.8 %all-reduce.5.cloned.1.call-start = ((), (), s32[]{:S(2)}) async-start(), calls=%async_computation.2 | async-start | bytes 37748736 | tf_op jit(solution)/shard_map/psum | solution.py:73
  306.0 482.7 %copy-start.20 = (f32[2304]{0:T(1024)S(1)}, f32[2304]{0:T(1024)}, u32[]{:S(2)}) copy-start(f32[2304]{0:T(1024)} %get-tuple-element.196) | copy-start | bytes 27652
  306.0 1088.2 %all-reduce.7.cloned.1.call-start = ((), (), s32[]{:S(2)}) async-start(), calls=%async_computation.3 | async-start | bytes 37748736 | tf_op jit(solution)/shard_map/psum | solution.py:79
  788.7 14.6 copy-start.24
  975.8 426.1 %copy-start.19 = (f32[2304]{0:T(1024)S(1)}, f32[2304]{0:T(1024)}, u32[]{:S(2)}) copy-start(f32[2304]{0:T(1024)} %get-tuple-element.194) | copy-start | bytes 27652
  975.8 508.1 %all-gather.11.cloned.1.call-start = ((), (), s32[]{:S(2)}) async-start(), calls=%async_computation.5 | async-start | bytes 10485760 | tf_op jit(solution)/shard_map/all_gather | solution.py:105
  1401.9 10.9 copy-start.23
  1412.7 10.2 copy-start.4
  1412.8 14.2 copy-start.9
  1426.9 114.6 %all-gather.9.cloned.1.call-start = ((), (), s32[]{:S(2)}) async-start(), calls=%async_computation.4 | async-start | bytes 10485760 | tf_op jit(solution)/shard_map/all_gather | solution.py:104
  1429.4 8.7 copy-start.27
  1443.4 1003.2 %all-reduce.9.cloned.1.call-start = ((), (), s32[]{:S(2)}) async-start(), calls=%async_computation.6 | async-start | bytes 37748736 | tf_op jit(solution)/shard_map/psum | solution.py:73
  1450.5 14.2 copy-start.26
  1688.0 766.2 %copy-start.18 = (f32[2304]{0:T(1024)S(1)}, f32[2304]{0:T(1024)}, u32[]{:S(2)}) copy-start(f32[2304]{0:T(1024)} %get-tuple-element.192) | copy-start | bytes 27652
  1688.0 1371.8 %all-reduce.11.cloned.1.call-start = ((), (), s32[]{:S(2)}) async-start(), calls=%async_computation.7 | async-start | bytes 37748736 | tf_op jit(solution)/shard_map/psum | solution.py:79
  2454.3 14.6 copy-start.22
  2641.4 6.4 copy-start.11
  2651.0 11.3 copy-start.17
  2675.6 391.9 %copy-start.21 = (f32[2304]{0:T(1024)S(1)}, f32[2304]{0:T(1024)}, u32[]{:S(2)}) copy-start(f32[2304]{0:T(1024)} %get-tuple-element.191) | copy-start | bytes 27652
  (43 other events, 178.6 us)
Sparse Core Ops, SparseCore 0:
  41.7 58.5 all-gather.4
  101.8 55.7 all-gather.6
  306.1 474.8 all-reduce.4
  975.9 418.2 all-reduce.6
  1427.1 56.7 all-gather.10
  1485.8 55.7 all-gather.8
  1688.1 758.3 all-reduce.8
  2641.6 418.2 all-reduce.10
where the time goes:
time: 3100 us; the launch traced here: 3090 us
  waiting for transfers between devices  2150 us (69%)
  matrix products  601 us (19%)
  other arithmetic  185 us (6%)
  local copies, waits for them, and re-layouts  131 us (4%)
    psum x2, waiting for transfers between devices, finish_layer(): lax.psum(jnp.dot(attn_rows, w_o, preferred_element_type=jnp.float32), 'tp')  1230 us
    psum x2, waiting for transfers between devices, finish_layer(): lax.psum(jnp.dot(act_rows, w_down, preferred_element_type=jnp.float32), '...  803 us
    dot_general x2, matrix products, finish_layer(): up_proj = jnp.dot(normed, w_up, preferred_element_type=jnp.float32)  130 us
    dot_general x2, matrix products, finish_layer(): jnp.dot(act_rows, w_down, preferred_element_type=jnp.float32)  113 us
    dot_general x2, matrix products, finish_layer(): gate_proj = jnp.dot(normed, w_gate, preferred_element_type=jnp.float32)  102 us
    dot_general x16, matrix products, loop_body(): jnp.einsum('hgqu,uhd->hgqd', prob_blk.astype(jnp.bfloat16), val_blk, pref...  82 us
    dot_general x16, matrix products, loop_body(): jnp.einsum('qhgd,uhd->hgqu', queries, key_blk, preferred_element_type=jnp...  78 us
    reduce_sum x8, other arithmetic, rms_scale(): mean_sq = jnp.mean(values * values, axis=-1, keepdims=True)  68.7 us
  transfers between devices with their start and end apart: 8, of which 7 were waited for; matrix products, arithmetic and copies ran while one was open for 5% of the time, Pallas kernels for 0%

commit v1 on v0

v1 whole, which is shorter than its diff:
```python
import functools

import jax
import jax.numpy as jnp
from jax import lax
from jax.experimental import pallas as pl
from jax.experimental.pallas import tpu as pltpu
from jax.sharding import PartitionSpec as P


THETAS = (10000.0, 1000000.0)
EPS = 1e-6
NEG_BIG = -1e30
LOG2E = 1.4426950408889634
F32 = jnp.float32
BF16 = jnp.bfloat16
VMEM_LIMIT = 67043328
ANY = pl.BlockSpec(memory_space=pl.ANY)


def rms_scale(values, gain):
    mean_sq = jnp.mean(values * values, axis=-1, keepdims=True)
    return values * lax.rsqrt(mean_sq + EPS) * (1.0 + gain)


def once(shape, index_map):
    return pl.BlockSpec(shape, index_map, pipeline_mode=pl.Buffered(1))


def run_kernel(kernel, args, in_specs, out_shape, out_specs, grid, scalars=(), deps=(), scratch=(), flops=0, nbytes=0, aliases=None):
    n_scalar = len(scalars)
    n_in = len(args)
    n_dep = len(deps)

    def body(*refs):
        head = refs[: n_scalar + n_in]
        tail = refs[n_scalar + n_in + n_dep:]
        kernel(*head, *tail)

    return pl.pallas_call(
        body,
        out_shape=out_shape,
        grid_spec=pltpu.PrefetchScalarGridSpec(
            num_scalar_prefetch=n_scalar,
            grid=grid,
            in_specs=list(in_specs) + [ANY] * n_dep,
            out_specs=out_specs,
            scratch_shapes=list(scratch),
        ),
        compiler_params=pltpu.CompilerParams(vmem_limit_bytes=VMEM_LIMIT, dimension_semantics=("arbitrary",) * len(grid)),
        cost_estimate=pl.CostEstimate(flops=int(flops), bytes_accessed=int(nbytes), transcendentals=0),
        input_output_aliases=aliases or {},
    )(*scalars, *args, *deps)


def sds(shape, dtype):
    return jax.ShapeDtypeStruct(shape, dtype)


def project_rows(x_rows, w_q, w_k, w_v, gain, qk_gain, base_tab, off_tab, q_out, kv_out, row0, head_dim):
    normed = rms_scale(x_rows.astype(F32), gain).astype(BF16)
    rows = x_rows.shape[0]
    half = head_dim // 2
    cos_off, sin_off = off_tab[0], off_tab[1]
    cosines, sines = [], []
    for g in range(rows // 32):
        cos_base, sin_base = base_tab[0, g:g + 1, :], base_tab[1, g:g + 1, :]
        cosines.append(cos_base * cos_off - sin_base * sin_off)
        sines.append(sin_base * cos_off + cos_base * sin_off)
    cosine = jnp.concatenate(cosines, axis=0)
    sine_val = jnp.concatenate(sines, axis=0)

    def rotate(proj, head_gain):
        normed_head = rms_scale(proj, head_gain)
        lower, upper = normed_head[:, :half], normed_head[:, half:]
        return jnp.concatenate([lower * cosine - upper * sine_val, upper * cosine + lower * sine_val], axis=1).astype(BF16)

    n_kv = w_k.shape[-1] // head_dim
    for h in range(w_q.shape[-1] // head_dim):
        cols = slice(h * head_dim, (h + 1) * head_dim)
        proj = jnp.dot(normed, w_q[:, cols], preferred_element_type=F32)
        q_out[row0:row0 + rows, cols] = rotate(proj, qk_gain[0:1, :])
    for h in range(n_kv):
        cols = slice(h * head_dim, (h + 1) * head_dim)
        proj = jnp.dot(normed, w_k[:, cols], preferred_element_type=F32)
        kv_out[row0:row0 + rows, cols] = rotate(proj, qk_gain[1:2, :])
    for h in range(n_kv):
        cols = slice(h * head_dim, (h + 1) * head_dim)
        out_cols = slice((n_kv + h) * head_dim, (n_kv + h + 1) * head_dim)
        kv_out[row0:row0 + rows, out_cols] = jnp.dot(normed, w_v[:, cols], preferred_element_type=F32).astype(BF16)


def weight_specs(layer, w_q, w_k, w_v, norm_gain, qk_gain):
    return [
        once((None,) + w_q.shape[1:], lambda i, *s: (layer, 0, 0)),
        once((None,) + w_k.shape[1:], lambda i, *s: (layer, 0, 0)),
        once((None,) + w_v.shape[1:], lambda i, *s: (layer, 0, 0)),
        once((None,) + norm_gain.shape[1:], lambda i, *s: (layer, 0, 0)),
        once((None,) + qk_gain.shape[1:], lambda i, *s: (layer, 0, 0)),
    ]


def qkv_from_rows(layer, x, row0, rows, weights, tabs, deps):
    w_q, w_k, _, _, qk_gain = weights
    base_tab, off_tab = tabs
    head_dim = qk_gain.shape[-1]
    width = x.shape[1]
    bm = 256
    b0 = row0 // bm

    def kernel(x_ref, wq, wk, wv, ng, qg, bt, ot, q_out, kv_out):
        project_rows(x_ref[...], wq, wk, wv, ng[0:1, :], qg, bt, ot, q_out, kv_out, 0, head_dim)

    nq, nkv = w_q.shape[-1], 2 * w_k.shape[-1]
    return run_kernel(
        kernel, (x, *weights, base_tab, off_tab),
        [pl.BlockSpec((bm, width), lambda i: (b0 + i, 0))] + weight_specs(layer, *weights)
        + [pl.BlockSpec((None, 2, bm // 32, head_dim // 2), lambda i: (layer, 0, b0 + i, 0)),
           once((None, 2, 32, head_dim // 2), lambda i: (layer, 0, 0, 0))],
        (sds((rows, nq), BF16), sds((rows, nkv), BF16)),
        [pl.BlockSpec((bm, nq), lambda i: (i, 0)), pl.BlockSpec((bm, nkv), lambda i: (i, 0))],
        (rows // bm,), deps=deps,
        flops=2 * rows * width * (nq + nkv), nbytes=2 * width * (nq + nkv + rows),
    )


def qkv_from_pieces(layer, tp_id, x_keep, x_other, row0, weights, tabs, deps):
    w_q, w_k, _, _, qk_gain = weights
    base_tab, off_tab = tabs
    head_dim = qk_gain.shape[-1]
    bm, width = x_keep.shape
    b0 = row0 // bm

    def kernel(tp, keep_ref, other_ref, wq, wk, wv, ng, qg, bt, ot, q_out, kv_out, x_out):
        rows = jnp.where(pl.program_id(0) == 0, keep_ref[...], other_ref[...])
        x_out[...] = rows
        project_rows(rows, wq, wk, wv, ng[0:1, :], qg, bt, ot, q_out, kv_out, 0, head_dim)

    def half(i, tp):
        return lax.rem(i + tp[0], 2)

    nq, nkv = w_q.shape[-1], 2 * w_k.shape[-1]
    rows = 2 * bm
    return run_kernel(
        kernel, (x_keep, x_other, *weights, base_tab, off_tab),
        [once((bm, width), lambda i, tp: (0, 0)), once((bm, width), lambda i, tp: (0, 0))] + weight_specs(layer, *weights)
        + [pl.BlockSpec((None, 2, bm // 32, head_dim // 2), lambda i, tp: (layer, 0, b0 + half(i, tp), 0)),
           once((None, 2, 32, head_dim // 2), lambda i, tp: (layer, 0, 0, 0))],
        (sds((rows, nq), BF16), sds((rows, nkv), BF16), sds((rows, width), BF16)),
        [pl.BlockSpec((bm, nq), lambda i, tp: (half(i, tp), 0)), pl.BlockSpec((bm, nkv), lambda i, tp: (half(i, tp), 0)),
         pl.BlockSpec((bm, width), lambda i, tp: (half(i, tp), 0))],
        (2,), scalars=(tp_id,), deps=deps,
        flops=2 * rows * width * (nq + nkv), nbytes=2 * width * (nq + nkv + 2 * rows),
    )


def dot_t(a, b):
    return lax.dot_general(a, b, (((1,), (1,)), ((), ())), preferred_element_type=F32)


def local_attention(first, q, q_block, kv_blocks, head_dim, chunk, deps):
    nq = q.shape[1]
    nkv_heads = kv_blocks[0][0].shape[1] // (2 * head_dim)
    groups = nq // head_dim // nkv_heads
    factor = head_dim ** -0.5 * LOG2E
    sub = 256

    def kernel(first_ref, q_ref, ka, va, kb, vb, kc, vc, o_ref):
        key_refs, val_refs = (ka, kb, kc), (va, vb, vc)
        for g in range(groups):
            for r in range(chunk // sub):
                q_rows = q_ref[r * sub:(r + 1) * sub, g * head_dim:(g + 1) * head_dim]
                row = lax.broadcasted_iota(jnp.int32, (sub, chunk), 0) + r * sub
                col = lax.broadcasted_iota(jnp.int32, (sub, chunk), 1)
                scores = []
                for b in range(3):
                    s = dot_t(q_rows, key_refs[b][...])
                    if b == 0:
                        s = jnp.where(col > row, s, NEG_BIG)
                    if b == 2:
                        s = jnp.where(col <= row, s, NEG_BIG)
                    if kv_blocks[b][2]:
                        s = jnp.where(first_ref[0] == 1, NEG_BIG, s)
                    scores.append(s)
                top = functools.reduce(jnp.maximum, [jnp.max(s, axis=1, keepdims=True) for s in scores])
                total = jnp.zeros((sub, 1), F32)
                out = jnp.zeros((sub, head_dim), F32)
                for b in range(3):
                    p = jnp.exp2((scores[b] - top) * factor)
                    total = total + jnp.sum(p, axis=1, keepdims=True)
                    out = out + jnp.dot(p.astype(BF16), val_refs[b][...], preferred_element_type=F32)
                o_ref[r * sub:(r + 1) * sub, g * head_dim:(g + 1) * head_dim] = (out / total).astype(BF16)

    specs = [pl.BlockSpec((chunk, groups * head_dim), lambda i, f: (q_block, i))]
    args = [q]
    for array, block, _ in kv_blocks:
        specs.append(pl.BlockSpec((chunk, head_dim), lambda i, f, block=block: (block, i)))
        specs.append(pl.BlockSpec((chunk, head_dim), lambda i, f, block=block: (block, nkv_heads + i)))
        args += [array, array]
    return run_kernel(
        kernel, args, specs, sds((chunk, nq), BF16),
        pl.BlockSpec((chunk, groups * head_dim), lambda i, f: (0, i)), (nkv_heads,),
        scalars=(first,), deps=deps, flops=4 * chunk * 3 * chunk * nq, nbytes=10 * chunk * nq,
    )


def global_attention(rank, q, gathered, n_own, head_dim, chunk, deps):
    nq = q.shape[1]
    nkv_heads = gathered[0].shape[1] // (2 * head_dim)
    groups = nq // head_dim // nkv_heads
    n_chunk = len(gathered)
    factor = head_dim ** -0.5 * LOG2E
    sub = 256
    n_sub = groups * chunk // sub

    def kernel(rank_ref, q_ref, *refs):
        kv_refs = refs[:n_chunk]
        o_ref, k_buf, v_buf, top_ref, total_ref, acc_ref, sems = refs[n_chunk:]
        g = pl.program_id(0)
        me = rank_ref[0]

        def copies(j, c):
            rows = pl.ds(pl.multiple_of(j * chunk, chunk), chunk)
            return (
                pltpu.make_async_copy(kv_refs[c].at[rows, pl.ds(pl.multiple_of(g * head_dim, head_dim), head_dim)], k_buf.at[c], sems.at[0, c]),
                pltpu.make_async_copy(kv_refs[c].at[rows, pl.ds(pl.multiple_of((nkv_heads + g) * head_dim, head_dim), head_dim)], v_buf.at[c], sems.at[1, c]),
            )

        def start(j, c):
            for copy in copies(j, c):
                copy.start()

        def wait(j, c):
            for copy in copies(j, c):
                copy.wait()

        def step(c, diagonal):
            for r in range(n_sub):
                head, part = divmod(r, chunk // sub)
                rows = slice(r * sub, (r + 1) * sub)
                q_rows = q_ref[part * sub:(part + 1) * sub, head * head_dim:(head + 1) * head_dim]
                s = dot_t(q_rows, k_buf[c])
                if diagonal:
                    row = lax.broadcasted_iota(jnp.int32, (sub, chunk), 0) + part * sub
                    col = lax.broadcasted_iota(jnp.int32, (sub, chunk), 1)
                    s = jnp.where(col <= row, s, NEG_BIG)
                old = top_ref[rows, 0:1]
                new = jnp.maximum(old, jnp.max(s, axis=1, keepdims=True))
                alpha = jnp.exp2((old - new) * factor)
                p = jnp.exp2((s - new) * factor)
                total_ref[rows, 0:1] = total_ref[rows, 0:1] * alpha + jnp.sum(p, axis=1, keepdims=True)
                acc_ref[rows, :] = acc_ref[rows, :] * alpha + jnp.dot(p.astype(BF16), v_buf[c], preferred_element_type=F32)
                top_ref[rows, 0:1] = new

        for c in range(n_chunk):
            start(0, c)
        top_ref[...] = jnp.full_like(top_ref, NEG_BIG)
        total_ref[...] = jnp.zeros_like(total_ref)
        acc_ref[...] = jnp.zeros_like(acc_ref)

        @pl.loop(0, me)
        def _(j):
            for c in range(n_chunk):
                wait(j, c)
                step(c, False)
                start(j + 1, c)

        for c in range(n_chunk):
            wait(me, c)
            if c < n_own:
                step(c, c == n_own - 1)
        for r in range(n_sub):
            head, part = divmod(r, chunk // sub)
            rows = slice(r * sub, (r + 1) * sub)
            o_ref[part * sub:(part + 1) * sub, head * head_dim:(head + 1) * head_dim] = (acc_ref[rows, :] / total_ref[rows, 0:1]).astype(BF16)

    return run_kernel(
        kernel, (q, *gathered),
        [pl.BlockSpec((chunk, groups * head_dim), lambda i, f: (0, i))] + [ANY] * n_chunk,
        sds((chunk, nq), BF16), pl.BlockSpec((chunk, groups * head_dim), lambda i, f: (0, i)), (nkv_heads,),
        scalars=(rank,), deps=deps,
        scratch=[pltpu.VMEM((n_chunk, chunk, head_dim), BF16), pltpu.VMEM((n_chunk, chunk, head_dim), BF16),
                 pltpu.VMEM((groups * chunk, 128), F32), pltpu.VMEM((groups * chunk, 128), F32),
                 pltpu.VMEM((groups * chunk, head_dim), F32), pltpu.SemaphoreType.DMA((2, n_chunk))],
        flops=4 * chunk * (2 * n_chunk * chunk) * nq, nbytes=16 * chunk * nq,
    )


def out_project(layer, tp_id, o_own, o_other, w_o, w_other, x, x_block, norm_gain, deps):
    chunk, k_own = o_own.shape
    width = w_o.shape[-1]
    bm = chunk // 2
    sub = 128

    def half(i, tp):
        return lax.rem(i + 1 + tp[0], 2)

    def kernel(tp, own_ref, oth_ref, w_own, w_oth, x_ref, ng, r_ref, m_ref):
        for part in range(bm // sub):
            rows = slice(part * sub, (part + 1) * sub)
            attn = jnp.dot(own_ref[rows, :], w_own[...], preferred_element_type=F32) + jnp.dot(oth_ref[rows, :], w_oth[...], preferred_element_type=F32)
            resid = (x_ref[rows, :].astype(F32) + rms_scale(attn, ng[1:2, :])).astype(BF16)
            r_ref[rows, :] = resid
            m_ref[rows, :] = rms_scale(resid.astype(F32), ng[2:3, :]).astype(BF16)

    return run_kernel(
        kernel, (o_own, o_other, w_o, w_other, x, norm_gain),
        [pl.BlockSpec((bm, k_own), lambda i, tp: (half(i, tp), 0)), pl.BlockSpec((bm, k_own), lambda i, tp: (half(i, tp), 0)),
         once((None, k_own, width), lambda i, tp: (layer, 0, 0)), once((k_own, width), lambda i, tp: (0, 0)),
         pl.BlockSpec((bm, width), lambda i, tp: (2 * x_block + half(i, tp), 0)),
         once((None,) + norm_gain.shape[1:], lambda i, tp: (layer, 0, 0))],
        (sds((chunk, width), BF16), sds((chunk, width), BF16)),
        [pl.BlockSpec((bm, width), lambda i, tp: (i, 0)), pl.BlockSpec((bm, width), lambda i, tp: (i, 0))],
        (2,), scalars=(tp_id,), deps=deps,
        flops=4 * chunk * k_own * width, nbytes=4 * k_own * width + 8 * chunk * width,
    )


def mlp_partial(layer, m, w_gate, w_up, w_down, deps):
    chunk, width = m.shape
    ff = w_gate.shape[-1]
    bf = 512
    bm = chunk // 2
    steps = ff // bf

    def kernel(m_ref, wg, wu, wd, send_ref, keep_ref):
        step = pl.program_id(0)
        for part, out_ref in ((0, send_ref), (1, keep_ref)):
            rows = m_ref[part * bm:(part + 1) * bm, :]
            gate = jnp.dot(rows, wg[...], preferred_element_type=F32)
            up = jnp.dot(rows, wu[...], preferred_element_type=F32)
            act = (jax.nn.gelu(gate, approximate=True) * up).astype(BF16)

            @pl.when(step == 0)
            def _():
                out_ref[...] = jnp.dot(act, wd[...], preferred_element_type=F32)

            @pl.when(step > 0)
            def _():
                out_ref[...] += jnp.dot(act, wd[...], preferred_element_type=F32)

    return run_kernel(
        kernel, (m, w_gate, w_up, w_down),
        [once((chunk, width), lambda i: (0, 0)),
         pl.BlockSpec((None, width, bf), lambda i: (layer, 0, i)), pl.BlockSpec((None, width, bf), lambda i: (layer, 0, i)),
         pl.BlockSpec((None, bf, width), lambda i: (layer, i, 0))],
        (sds((bm, width), F32), sds((bm, width), F32)),
        [pl.BlockSpec((bm, width), lambda i: (0, 0)), pl.BlockSpec((bm, width), lambda i: (0, 0))],
        (steps,), deps=deps, flops=6 * chunk * width * ff, nbytes=6 * width * ff + 6 * chunk * width,
    )


def finish_rows(layer, kept, received, r, norm_gain, deps):
    rows, width = kept.shape
    bm = 128
    skip = rows // bm

    def kernel(kept_ref, recv_ref, r_ref, ng, x_ref):
        x_ref[...] = (r_ref[...].astype(F32) + rms_scale(kept_ref[...] + recv_ref[...], ng[3:4, :])).astype(BF16)

    return run_kernel(
        kernel, (kept, received, r, norm_gain),
        [pl.BlockSpec((bm, width), lambda i: (i, 0)), pl.BlockSpec((bm, width), lambda i: (i, 0)),
         pl.BlockSpec((bm, width), lambda i: (skip + i, 0)), once((None,) + norm_gain.shape[1:], lambda i: (layer, 0, 0))],
        sds((rows, width), BF16), pl.BlockSpec((bm, width), lambda i: (i, 0)), (rows // bm,), deps=deps,
        flops=20 * rows * width, nbytes=12 * rows * width,
    )


def place_rows(tp_id, x_keep, x_other, row0, total_rows, target, deps):
    bm, width = x_keep.shape
    b0 = row0 // bm

    def half(i, tp):
        return lax.rem(i + tp[0], 2)

    def kernel(tp, keep_ref, other_ref, *refs):
        refs[-1][...] = jnp.where(pl.program_id(0) == 0, keep_ref[...], other_ref[...])

    specs = [once((bm, width), lambda i, tp: (0, 0)), once((bm, width), lambda i, tp: (0, 0))]
    args = [x_keep, x_other]
    aliases = None
    if target is not None:
        specs.append(ANY)
        args.append(target)
        aliases = {3: 0}
    return run_kernel(
        kernel, args, specs, sds((total_rows, width), BF16),
        pl.BlockSpec((bm, width), lambda i, tp: (b0 + half(i, tp), 0)), (2,), scalars=(tp_id,), deps=deps, aliases=aliases,
        flops=bm * width, nbytes=8 * bm * width,
    )


SEQUENCE = (
    ("swap", 0, 0), ("qkv", 0, 1), ("halo", 0, 0), ("qkv", 0, 0), ("attn", 0, 2), ("attn", 0, 3), ("attn", 0, 0), ("attn", 0, 1),
    ("wo", 0, 2), ("mlp", 0, 2), ("wo", 0, 3), ("mlp", 0, 3), ("wo", 0, 0), ("mlp", 0, 0), ("post", 0, 2),
    ("wo", 0, 1), ("mlp", 0, 1), ("post", 0, 3), ("post", 0, 0), ("cache", 0, 0), ("qkv", 1, 2), ("post", 0, 1), ("swap", 1, 0),
    ("qkv", 1, 3), ("qkv", 1, 0), ("qkv", 1, 1),
    ("attn", 1, 2), ("attn", 1, 3), ("wo", 1, 2), ("mlp", 1, 2), ("attn", 1, 0), ("wo", 1, 3), ("mlp", 1, 3), ("attn", 1, 1),
    ("cache", 1, 0), ("wo", 1, 0), ("mlp", 1, 0), ("post", 1, 2), ("wo", 1, 1), ("mlp", 1, 1), ("post", 1, 3), ("post", 1, 0),
    ("place", 1, 2), ("place", 1, 3), ("post", 1, 1), ("place", 1, 0), ("place", 1, 1),
)


def solution(mesh):
    cp_size = mesh.shape['cp']
    tp_size = mesh.shape['tp']
    assert tp_size == 2
    row_spec = P(('dp', 'cp'), None)
    col_spec = P(None, None, 'tp')
    row_w_spec = P(None, 'tp', None)
    cache_spec = P(None, ('dp', 'cp'), 'tp', None)
    swap = [(0, 1), (1, 0)]

    def device_fn(hidden, positions, w_q, w_k, w_v, w_o, w_gate, w_up, w_down, norm_gain, qk_gain):
        tok_rows, width = hidden.shape
        head_dim = qk_gain.shape[-1]
        half_dim = head_dim // 2
        kv_width = w_k.shape[-1]
        chunk = 512
        n_chunk = tok_rows // chunk
        high = tok_rows // 2
        tp_id = lax.axis_index('tp').astype(jnp.int32).reshape(1)
        cp_id = lax.axis_index('cp').astype(jnp.int32)
        rank = cp_id.reshape(1)
        first = (cp_id == 0).astype(jnp.int32).reshape(1)

        def exchange(value):
            return lax.ppermute(value, 'tp', swap)

        theta_col = jnp.array(THETAS, F32)[:, None]
        inv_freq = theta_col ** (-(jnp.arange(half_dim, dtype=F32) * 2.0) / head_dim)[None, :]
        base_pos = (positions[0] + 32 * jnp.arange(tok_rows // 32, dtype=jnp.int32)).astype(F32)
        base_ang = base_pos[None, :, None] * inv_freq[:, None, :]
        off_ang = jnp.arange(32, dtype=F32)[None, :, None] * inv_freq[:, None, :]
        tabs = (jnp.stack([jnp.cos(base_ang), jnp.sin(base_ang)], axis=1), jnp.stack([jnp.cos(off_ang), jnp.sin(off_ang)], axis=1))

        quarter = w_o.shape[1] // cp_size
        qkv_weights = (w_q, w_k, w_v, norm_gain, qk_gain)
        w_other, q_rot, kv_own, kv_all, x_mid = {}, {}, {}, {}, {}
        o_own, o_oth, r_rows, m_rows, kept, recv, x_keep, x_oth = {}, {}, {}, {}, {}, {}, {}, {}
        halo = None
        out = None
        caches = [jnp.zeros((2, tok_rows, kv_width // head_dim, head_dim), BF16) for _ in range(2)]
        deps = ()

        for kind, layer, c in SEQUENCE:
            if kind == "swap":
                piece = lax.dynamic_slice(w_o, (layer, cp_id * quarter, 0), (1, quarter, width))[0]
                if deps:
                    piece, _ = lax.optimization_barrier((piece, deps[0]))
                w_other[layer] = lax.all_gather(exchange(piece), 'cp', axis=0, tiled=True)
                continue
            if kind == "halo":
                halo = lax.ppermute(kv_own[0, 1], 'cp', [(i, i + 1) for i in range(cp_size - 1)])
                continue
            if kind == "cache":
                pieces = [(kv_own[0, b], b * high) for b in range(2)] if layer == 0 else [(kv_own[1, b], b * chunk) for b in range(n_chunk)]
                tied = lax.optimization_barrier(tuple(p for p, _ in pieces) + tuple(deps))[: len(pieces)]
                for which in range(2):
                    for piece, (_, row) in zip(tied, pieces):
                        part = piece[:, which * kv_width:(which + 1) * kv_width].reshape(1, piece.shape[0], kv_width // head_dim, head_dim)
                        caches[which] = lax.dynamic_update_slice(caches[which], part, (layer, row, 0, 0))
                deps = (*deps, *caches)
                continue
            if kind == "qkv" and layer == 0:
                q_rot[0, c], kv_own[0, c] = qkv_from_rows(0, hidden, c * high, high, qkv_weights, tabs, deps)
                result = q_rot[0, c]
            elif kind == "qkv":
                q_rot[1, c], kv_own[1, c], x_mid[c] = qkv_from_pieces(1, tp_id, x_keep[0, c], x_oth[0, c], c * chunk, qkv_weights, tabs, deps)
                kv_all[c] = lax.all_gather(kv_own[1, c], 'cp', axis=0, tiled=True)
                result = q_rot[1, c]
            elif kind == "attn" and layer == 0:
                per = high // chunk
                blocks = [(kv_own[0, b // per], b % per, False) if b >= 0 else (halo, b + per, True) for b in (c - 2, c - 1, c)]
                result = o_own[c] = local_attention(first, q_rot[0, c // per], c % per, blocks, head_dim, chunk, deps)
                o_oth[c] = exchange(result)
            elif kind == "attn":
                result = o_own[c] = global_attention(rank, q_rot[1, c], [kv_all[i] for i in range(n_chunk)], c + 1, head_dim, chunk, deps)
                o_oth[c] = exchange(result)
            elif kind == "wo":
                x, x_block = (hidden, c) if layer == 0 else (x_mid[c], 0)
                r_rows[c], m_rows[c] = out_project(layer, tp_id, o_own[c], o_oth[c], w_o, w_other[layer], x, x_block, norm_gain, deps)
                result = r_rows[c]
            elif kind == "mlp":
                send, kept[c] = mlp_partial(layer, m_rows[c], w_gate, w_up, w_down, deps)
                recv[c] = exchange(send)
                result = kept[c]
            elif kind == "post":
                result = x_keep[layer, c] = finish_rows(layer, kept[c], recv[c], r_rows[c], norm_gain, deps)
                x_oth[layer, c] = exchange(result)
            elif kind == "place":
                result = out = place_rows(tp_id, x_keep[1, c], x_oth[1, c], c * chunk, tok_rows, out, deps if out is None or deps[0] is not out else ())
            deps = (result,)
        return out, caches[0], caches[1]

    return jax.shard_map(
        device_fn,
        mesh=mesh,
        in_specs=(row_spec, P(('dp', 'cp')), col_spec, col_spec, col_spec, row_w_spec, col_spec, col_spec, row_w_spec, P(), P()),
        out_specs=(row_spec, cache_spec, cache_spec),
        check_vma=False,
    )
```

time: 3100 us -> 1230 us (0.40)
  the two profiles are of different devices: /device:TPU:0 before, /device:TPU:3 now
where the time goes in v1:
time: 1230 us
  Pallas kernels  826 us (67%)
  waiting for transfers between devices  309 us (25%)
  local copies, waits for them, and re-layouts  54.7 us (4%)
  starting transfers between devices  21.8 us (2%)
  between operations  14.6 us (1%)
    pallas_call x42, Pallas kernels, run_kernel(): pl.pallas_call(body, out_shape=out_shape, grid_spec=pltpu.PrefetchScalarG...  826 us
    ppermute x26, waiting for transfers between devices, exchange(): return lax.ppermute(value, 'tp', swap)  259 us
    all_gather x4, waiting for transfers between devices, device_fn(): kv_all[c] = lax.all_gather(kv_own[1, c], 'cp', axis=0, tiled=True)  49.8 us
    dynamic_update_slice x12, local copies, waits for them, and re-layouts, device_fn(): lax.dynamic_update_slice(caches[which], part, (layer, row, 0, 0))  32 us
  transfers between devices with their start and end apart: 33, of which 13 were waited for; matrix products, arithmetic and copies ran while one was open for 4% of the time, Pallas kernels for 66%

profile of v1, /device:TPU:3, one launch (start us, length us, event | category | flops | bytes accessed | tf_op | source)
XLA Modules:
  0.0 1228.4 jit_solution(12713635393147399357)
XLA Ops:
  11.3 25.6 %collective-permute-done.2 = bf16[256,2304]{1,0:T(8,128)(2,1)S(1)} collective-permute-done((bf16[256,2304]{1,0:T(8,128)(2,1)S(1)}, bf16[256,2304]{1,0:T(8,128)(2,1)S(1)}, u32[]{:S(2)}, u32[]{:S(2)}) %collective-permute-start.2) | collective-permute-done | bytes 1179680 | tf_op jit(solution)/shard_map/ppermute | solution.py:429
  41.7 17.6 %shard_map.139 = (bf16[1024,1024]{1,0:T(8,128)(2,1)}, bf16[1024,1024]{1,0:T(8,128)(2,1)}) custom-call(bf16[2048,2304]{1,0:T(8,128)(2,1)} %refs_5_.15, bf16[2,2304,1024]{2,1,0:T(8,128)(2,1)} %refs_3_.47, bf16[2,2304,512]{2,1,0:T(8,128)(2,1)} %refs_4_.11, bf16[2,2304,512]{2,1,0:T(8,128)(2,1)} %refs_5_.19, f32[2,4,2304]{2,1,0:T(4,128)} %refs_3_.59, ...), custom_call_target="tpu_custom_call" | custom-call | flops 9663676416 | bytes 14155776 | tf_op jit(solution)/shard_map/pallas_call | solution.py:40
  60.9 16.9 %shard_map.140 = (bf16[1024,1024]{1,0:T(8,128)(2,1)}, bf16[1024,1024]{1,0:T(8,128)(2,1)}) custom-call(bf16[2048,2304]{1,0:T(8,128)(2,1)} %refs_5_.15, bf16[2,2304,1024]{2,1,0:T(8,128)(2,1)} %refs_3_.47, bf16[2,2304,512]{2,1,0:T(8,128)(2,1)} %refs_4_.11, bf16[2,2304,512]{2,1,0:T(8,128)(2,1)} %refs_5_.19, f32[2,4,2304]{2,1,0:T(4,128)} %refs_3_.59, ...), custom_call_target="tpu_custom_call" | custom-call | flops 9663676416 | bytes 14155776 | tf_op jit(solution)/shard_map/pallas_call | solution.py:40
  123.5 46.0 %shard_map.146 = (f32[256,2304]{1,0:T(8,128)}, f32[256,2304]{1,0:T(8,128)}) custom-call(bf16[512,2304]{1,0:T(8,128)(2,1)} %get-tuple-element.62.refs_0_, bf16[2,2304,4608]{2,1,0:T(8,128)(2,1)} %refs_1_.19, bf16[2,2304,4608]{2,1,0:T(8,128)(2,1)} %refs_2_.19, bf16[2,4608,2304]{2,1,0:T(8,128)(2,1)} %refs_3_.56, bf16[512,2304]{1,0:T(8,128)(2,1)} %get-tuple-element.63.refs_4_.refs_2_), custom_call_target="tpu_custom_call" | custom-call | flops 32614907904 | bytes 70778880 | tf_op jit(solution)/shard_map/pallas_call | solution.py:40
  183.5 45.8 %shard_map.148 = (f32[256,2304]{1,0:T(8,128)}, f32[256,2304]{1,0:T(8,128)}) custom-call(bf16[512,2304]{1,0:T(8,128)(2,1)} %get-tuple-element.66.refs_0_, bf16[2,2304,4608]{2,1,0:T(8,128)(2,1)} %refs_1_.19, bf16[2,2304,4608]{2,1,0:T(8,128)(2,1)} %refs_2_.19, bf16[2,4608,2304]{2,1,0:T(8,128)(2,1)} %refs_3_.56, bf16[512,2304]{1,0:T(8,128)(2,1)} %get-tuple-element.67.refs_4_.refs_2_), custom_call_target="tpu_custom_call" | custom-call | flops 32614907904 | bytes 70778880 | tf_op jit(solution)/shard_map/pallas_call | solution.py:40
  242.2 46.2 %shard_map.150 = (f32[256,2304]{1,0:T(8,128)}, f32[256,2304]{1,0:T(8,128)}) custom-call(bf16[512,2304]{1,0:T(8,128)(2,1)} %get-tuple-element.69.refs_0_, bf16[2,2304,4608]{2,1,0:T(8,128)(2,1)} %refs_1_.19, bf16[2,2304,4608]{2,1,0:T(8,128)(2,1)} %refs_2_.19, bf16[2,4608,2304]{2,1,0:T(8,128)(2,1)} %refs_3_.56, bf16[512,2304]{1,0:T(8,128)(2,1)} %get-tuple-element.70.refs_4_.refs_2_), custom_call_target="tpu_custom_call" | custom-call | flops 32614907904 | bytes 70778880 | tf_op jit(solution)/shard_map/pallas_call | solution.py:40
  306.5 46.3 %shard_map.153 = (f32[256,2304]{1,0:T(8,128)}, f32[256,2304]{1,0:T(8,128)}) custom-call(bf16[512,2304]{1,0:T(8,128)(2,1)} %get-tuple-element.72.refs_0_, bf16[2,2304,4608]{2,1,0:T(8,128)(2,1)} %refs_1_.19, bf16[2,2304,4608]{2,1,0:T(8,128)(2,1)} %refs_2_.19, bf16[2,4608,2304]{2,1,0:T(8,128)(2,1)} %refs_3_.56, bf16[512,2304]{1,0:T(8,128)(2,1)} %get-tuple-element.73.refs_4_.refs_2_), custom_call_target="tpu_custom_call" | custom-call | flops 32614907904 | bytes 70778880 | tf_op jit(solution)/shard_map/pallas_call | solution.py:40
  403.3 45.4 %collective-permute-done.7.refs_1_ = f32[256,2304]{1,0:T(8,128)} collective-permute-done((f32[256,2304]{1,0:T(8,128)}, f32[256,2304]{1,0:T(8,128)}, u32[]{:S(2)}, u32[]{:S(2)}) %collective-permute-start.7) | collective-permute-done | bytes 2359328 | tf_op jit(solution)/shard_map/ppermute | solution.py:429
  452.7 21.3 %collective-permute-done.13.refs_2_ = bf16[256,2304]{1,0:T(8,128)(2,1)} collective-permute-done((bf16[256,2304]{1,0:T(8,128)(2,1)}, bf16[256,2304]{1,0:T(8,128)(2,1)}, u32[]{:S(2)}, u32[]{:S(2)}) %collective-permute-start.13) | collective-permute-done | bytes 1179680 | tf_op jit(solution)/shard_map/ppermute | solution.py:429
  485.7 13.6 %collective-permute-done.12.refs_2_ = bf16[256,2304]{1,0:T(8,128)(2,1)} collective-permute-done((bf16[256,2304]{1,0:T(8,128)(2,1)}, bf16[256,2304]{1,0:T(8,128)(2,1)}, u32[]{:S(2)}, u32[]{:S(2)}) %collective-permute-start.12) | collective-permute-done | bytes 1179680 | tf_op jit(solution)/shard_map/ppermute | solution.py:429
  513.0 20.7 %collective-permute-done.11.refs_2_ = bf16[256,2304]{1,0:T(8,128)(2,1)} collective-permute-done((bf16[256,2304]{1,0:T(8,128)(2,1)}, bf16[256,2304]{1,0:T(8,128)(2,1)}, u32[]{:S(2)}, u32[]{:S(2)}) %collective-permute-start.11) | collective-permute-done | bytes 1179680 | tf_op jit(solution)/shard_map/ppermute | solution.py:429
  546.9 19.7 %collective-permute-done.15 = bf16[256,2304]{1,0:T(8,128)(2,1)S(1)} collective-permute-done((bf16[256,2304]{1,0:T(8,128)(2,1)}, bf16[256,2304]{1,0:T(8,128)(2,1)S(1)}, u32[]{:S(2)}, u32[]{:S(2)}) %collective-permute-start.15) | collective-permute-done | bytes 1179680 | tf_op jit(solution)/shard_map/ppermute | solution.py:429
  567.7 16.6 %all-gather.15.cloned.1.call-done.refs_5_ = bf16[2048,1024]{1,0:T(8,128)(2,1)} async-done(((bf16[512,1024]{1,0:T(8,128)(2,1)}), bf16[2048,1024]{1,0:T(8,128)(2,1)}) %all-gather.15.cloned.1.call-update) | async-done | bytes 4194320 | tf_op jit(solution)/shard_map/all_gather | solution.py:471
  584.3 33.1 %all-gather.11.cloned.1.call-done.refs_3_ = bf16[2048,1024]{1,0:T(8,128)(2,1)} async-done(((bf16[512,1024]{1,0:T(8,128)(2,1)}), bf16[2048,1024]{1,0:T(8,128)(2,1)}) %all-gather.11.cloned.1.call-update) | async-done | bytes 4194320 | tf_op jit(solution)/shard_map/all_gather | solution.py:471
  617.4 51.2 %shard_map.161.refs_6_.refs_1_ = bf16[512,1024]{1,0:T(8,128)(2,1)} custom-call(s32[1]{0:T(128)} %bitcast.1.refs_0_, bf16[512,1024]{1,0:T(8,128)(2,1)} %get-tuple-element.80.refs_4_.refs_1_, bf16[2048,1024]{1,0:T(8,128)(2,1)} %all-gather.9.cloned.1.call-done.refs_2_, bf16[2048,1024]{1,0:T(8,128)(2,1)} %all-gather.11.cloned.1.call-done.refs_3_, ...), custom_call_target="tpu_custom_call" | custom-call | flops 8589934592 | bytes 8388608 | tf_op jit(solution)/shard_map/pallas_call | solution.py:40
  670.1 54.2 %shard_map.162.refs_7_.refs_1_ = bf16[512,1024]{1,0:T(8,128)(2,1)} custom-call(s32[1]{0:T(128)} %bitcast.1.refs_0_, bf16[512,1024]{1,0:T(8,128)(2,1)} %get-tuple-element.81.refs_10_.refs_1_, bf16[2048,1024]{1,0:T(8,128)(2,1)} %all-gather.9.cloned.1.call-done.refs_2_, bf16[2048,1024]{1,0:T(8,128)(2,1)} %all-gather.11.cloned.1.call-done.refs_3_, ...), custom_call_target="tpu_custom_call" | custom-call | flops 8589934592 | bytes 8388608 | tf_op jit(solution)/shard_map/pallas_call | solution.py:40
  737.2 45.9 %shard_map.164 = (f32[256,2304]{1,0:T(8,128)}, f32[256,2304]{1,0:T(8,128)}) custom-call(bf16[512,2304]{1,0:T(8,128)(2,1)} %get-tuple-element.91.refs_0_, bf16[2,2304,4608]{2,1,0:T(8,128)(2,1)} %refs_1_.19, bf16[2,2304,4608]{2,1,0:T(8,128)(2,1)} %refs_2_.19, bf16[2,4608,2304]{2,1,0:T(8,128)(2,1)} %refs_3_.56, bf16[512,2304]{1,0:T(8,128)(2,1)} %get-tuple-element.92.refs_4_.refs_2_), custom_call_target="tpu_custom_call" | custom-call | flops 32614907904 | bytes 70778880 | tf_op jit(solution)/shard_map/pallas_call | solution.py:40
  783.1 45.1 %shard_map.165.refs_7_.refs_1_ = bf16[512,1024]{1,0:T(8,128)(2,1)} custom-call(s32[1]{0:T(128)} %bitcast.1.refs_0_, bf16[512,1024]{1,0:T(8,128)(2,1)} %get-tuple-element.82.refs_10_.refs_1_, bf16[2048,1024]{1,0:T(8,128)(2,1)} %all-gather.9.cloned.1.call-done.refs_2_, bf16[2048,1024]{1,0:T(8,128)(2,1)} %all-gather.11.cloned.1.call-done.refs_3_, ...), custom_call_target="tpu_custom_call" | custom-call | flops 8589934592 | bytes 8388608 | tf_op jit(solution)/shard_map/pallas_call | solution.py:40
  842.3 46.3 %shard_map.167 = (f32[256,2304]{1,0:T(8,128)}, f32[256,2304]{1,0:T(8,128)}) custom-call(bf16[512,2304]{1,0:T(8,128)(2,1)} %get-tuple-element.94.refs_0_, bf16[2,2304,4608]{2,1,0:T(8,128)(2,1)} %refs_1_.19, bf16[2,2304,4608]{2,1,0:T(8,128)(2,1)} %refs_2_.19, bf16[2,4608,2304]{2,1,0:T(8,128)(2,1)} %refs_3_.56, bf16[512,2304]{1,0:T(8,128)(2,1)} %get-tuple-element.95.refs_4_.refs_2_), custom_call_target="tpu_custom_call" | custom-call | flops 32614907904 | bytes 70778880 | tf_op jit(solution)/shard_map/pallas_call | solution.py:40
  888.6 48.1 %shard_map.168.refs_7_.refs_1_ = bf16[512,1024]{1,0:T(8,128)(2,1)} custom-call(s32[1]{0:T(128)} %bitcast.1.refs_0_, bf16[512,1024]{1,0:T(8,128)(2,1)} %get-tuple-element.83.refs_6_.refs_1_, bf16[2048,1024]{1,0:T(8,128)(2,1)} %all-gather.9.cloned.1.call-done.refs_2_, bf16[2048,1024]{1,0:T(8,128)(2,1)} %all-gather.11.cloned.1.call-done.refs_3_, ...), custom_call_target="tpu_custom_call" | custom-call | flops 8589934592 | bytes 8388608 | tf_op jit(solution)/shard_map/pallas_call | solution.py:40
  971.8 45.9 %shard_map.170 = (f32[256,2304]{1,0:T(8,128)}, f32[256,2304]{1,0:T(8,128)}) custom-call(bf16[512,2304]{1,0:T(8,128)(2,1)} %get-tuple-element.104.refs_0_, bf16[2,2304,4608]{2,1,0:T(8,128)(2,1)} %refs_1_.19, bf16[2,2304,4608]{2,1,0:T(8,128)(2,1)} %refs_2_.19, bf16[2,4608,2304]{2,1,0:T(8,128)(2,1)} %refs_3_.56, ...), custom_call_target="tpu_custom_call" | custom-call | flops 32614907904 | bytes 70778880 | tf_op jit(solution)/shard_map/pallas_call | solution.py:40
  1036.1 46.1 %shard_map.173 = (f32[256,2304]{1,0:T(8,128)}, f32[256,2304]{1,0:T(8,128)}) custom-call(bf16[512,2304]{1,0:T(8,128)(2,1)} %get-tuple-element.107.refs_0_, bf16[2,2304,4608]{2,1,0:T(8,128)(2,1)} %refs_1_.19, bf16[2,2304,4608]{2,1,0:T(8,128)(2,1)} %refs_2_.19, bf16[2,4608,2304]{2,1,0:T(8,128)(2,1)} %refs_3_.56, ...), custom_call_target="tpu_custom_call" | custom-call | flops 32614907904 | bytes 70778880 | tf_op jit(solution)/shard_map/pallas_call | solution.py:40
  1098.6 71.7 %collective-permute-done.23.refs_2_ = bf16[256,2304]{1,0:T(8,128)(2,1)} collective-permute-done((bf16[256,2304]{1,0:T(8,128)(2,1)}, bf16[256,2304]{1,0:T(8,128)(2,1)}, u32[]{:S(2)}, u32[]{:S(2)}) %collective-permute-start.23) | collective-permute-done | bytes 1179680 | tf_op jit(solution)/shard_map/ppermute | solution.py:429
  1173.4 19.5 %collective-permute-done.22.refs_2_ = bf16[256,2304]{1,0:T(8,128)(2,1)} collective-permute-done((bf16[256,2304]{1,0:T(8,128)(2,1)}, bf16[256,2304]{1,0:T(8,128)(2,1)}, u32[]{:S(2)}, u32[]{:S(2)}) %collective-permute-start.22) | collective-permute-done | bytes 1179680 | tf_op jit(solution)/shard_map/ppermute | solution.py:429
  (140 shorter events, 325.1 us)
Async XLA Ops:
  7.2 103.7 %all-gather.7.cloned.1.call-start = ((), (), s32[]{:S(2)}) async-start(), calls=%async_computation | async-start | bytes 5898240 | tf_op jit(solution)/shard_map/all_gather | solution.py:452
  37.9 529.7 %all-gather.13.cloned.1.call-start = ((), (), s32[]{:S(2)}) async-start(), calls=%async_computation.3 | async-start | bytes 5242880 | tf_op jit(solution)/shard_map/all_gather | solution.py:471
  93.7 77.0 %collective-permute-start.6 = (bf16[512,1024]{1,0:T(8,128)(2,1)}, bf16[512,1024]{1,0:T(8,128)(2,1)}, u32[]{:S(2)}, u32[]{:S(2)}) collective-permute-start(bf16[512,1024]{1,0:T(8,128)(2,1)} %shard_map.142.refs_8_.refs_1_), channel_id=1, source_target_pairs={{0,4},{4,0},{1,5},{5,1},{2,6},{6,2},{3,7},{7,3}} | collective-permute-start | bytes 3145736 | tf_op jit(solution)/shard_map/ppermute | solution.py:429
  101.5 128.1 %collective-permute-start.5 = (bf16[512,1024]{1,0:T(8,128)(2,1)}, bf16[512,1024]{1,0:T(8,128)(2,1)}, u32[]{:S(2)}, u32[]{:S(2)}) collective-permute-start(bf16[512,1024]{1,0:T(8,128)(2,1)} %shard_map.143.refs_8_.refs_1_), channel_id=1, source_target_pairs={{0,4},{4,0},{1,5},{5,1},{2,6},{6,2},{3,7},{7,3}} | collective-permute-start | bytes 3145736 | tf_op jit(solution)/shard_map/ppermute | solution.py:429
  110.6 183.2 %collective-permute-start.1 = (bf16[512,1024]{1,0:T(8,128)(2,1)}, bf16[512,1024]{1,0:T(8,128)(2,1)}, u32[]{:S(2)}, u32[]{:S(2)}) collective-permute-start(bf16[512,1024]{1,0:T(8,128)(2,1)} %shard_map.144.refs_7_.refs_1_), channel_id=1, source_target_pairs={{0,4},{4,0},{1,5},{5,1},{2,6},{6,2},{3,7},{7,3}} | collective-permute-start | bytes 3145736 | tf_op jit(solution)/shard_map/ppermute | solution.py:429
  169.5 120.2 %collective-permute-start.4 = (f32[256,2304]{1,0:T(8,128)}, f32[256,2304]{1,0:T(8,128)}, u32[]{:S(2)}, u32[]{:S(2)}) collective-permute-start(f32[256,2304]{1,0:T(8,128)} %get-tuple-element.65), channel_id=1, source_target_pairs={{0,4},{4,0},{1,5},{5,1},{2,6},{6,2},{3,7},{7,3}} | collective-permute-start | bytes 7077896 | tf_op jit(solution)/shard_map/ppermute | solution.py:429
  229.4 123.4 %collective-permute-start.10 = (f32[256,2304]{1,0:T(8,128)}, f32[256,2304]{1,0:T(8,128)}, u32[]{:S(2)}, u32[]{:S(2)}) collective-permute-start(f32[256,2304]{1,0:T(8,128)} %get-tuple-element.77), channel_id=1, source_target_pairs={{0,4},{4,0},{1,5},{5,1},{2,6},{6,2},{3,7},{7,3}} | collective-permute-start | bytes 7077896 | tf_op jit(solution)/shard_map/ppermute | solution.py:429
  293.6 94.9 %collective-permute-start.8 = (bf16[256,2304]{1,0:T(8,128)(2,1)}, bf16[256,2304]{1,0:T(8,128)(2,1)}, u32[]{:S(2)}, u32[]{:S(2)}) collective-permute-start(bf16[256,2304]{1,0:T(8,128)(2,1)} %shard_map.151.refs_7_.refs_1_), channel_id=1, source_target_pairs={{0,4},{4,0},{1,5},{5,1},{2,6},{6,2},{3,7},{7,3}} | collective-permute-start | bytes 3538952 | tf_op jit(solution)/shard_map/ppermute | solution.py:429
  400.5 167.2 %all-gather.9.cloned.1.call-start = ((), (), s32[]{:S(2)}) async-start(), calls=%async_computation.1 | async-start | bytes 5242880 | tf_op jit(solution)/shard_map/all_gather | solution.py:471
  401.8 72.1 %collective-permute-start.13 = (bf16[256,2304]{1,0:T(8,128)(2,1)}, bf16[256,2304]{1,0:T(8,128)(2,1)}, u32[]{:S(2)}, u32[]{:S(2)}) collective-permute-start(bf16[256,2304]{1,0:T(8,128)(2,1)} %shard_map.154.refs_4_.refs_1_), channel_id=1, source_target_pairs={{0,4},{4,0},{1,5},{5,1},{2,6},{6,2},{3,7},{7,3}} | collective-permute-start | bytes 3538952 | tf_op jit(solution)/shard_map/ppermute | solution.py:429
  402.1 97.2 %collective-permute-start.12 = (bf16[256,2304]{1,0:T(8,128)(2,1)}, bf16[256,2304]{1,0:T(8,128)(2,1)}, u32[]{:S(2)}, u32[]{:S(2)}) collective-permute-start(bf16[256,2304]{1,0:T(8,128)(2,1)} %shard_map.155.refs_10_.refs_1_), channel_id=1, source_target_pairs={{0,4},{4,0},{1,5},{5,1},{2,6},{6,2},{3,7},{7,3}} | collective-permute-start | bytes 3538952 | tf_op jit(solution)/shard_map/ppermute | solution.py:429
  511.0 73.3 %all-gather.15.cloned.1.call-start = ((), (), s32[]{:S(2)}) async-start(), calls=%async_computation.4 | async-start | bytes 5242880 | tf_op jit(solution)/shard_map/all_gather | solution.py:471
  511.6 105.8 %all-gather.11.cloned.1.call-start = ((), (), s32[]{:S(2)}) async-start(), calls=%async_computation.2 | async-start | bytes 5242880 | tf_op jit(solution)/shard_map/all_gather | solution.py:471
  545.4 178.9 %all-gather.17.cloned.1.call-start = ((), (), s32[]{:S(2)}) async-start(), calls=%async_computation.5 | async-start | bytes 5898240 | tf_op jit(solution)/shard_map/all_gather | solution.py:452
  724.2 105.4 %collective-permute-start.14 = (bf16[512,1024]{1,0:T(8,128)(2,1)}, bf16[512,1024]{1,0:T(8,128)(2,1)}, u32[]{:S(2)}, u32[]{:S(2)}) collective-permute-start(bf16[512,1024]{1,0:T(8,128)(2,1)} %shard_map.162.refs_7_.refs_1_), channel_id=1, source_target_pairs={{0,4},{4,0},{1,5},{5,1},{2,6},{6,2},{3,7},{7,3}} | collective-permute-start | bytes 3145736 | tf_op jit(solution)/shard_map/ppermute | solution.py:429
  828.2 131.0 %collective-permute-start.19 = (bf16[512,1024]{1,0:T(8,128)(2,1)}, bf16[512,1024]{1,0:T(8,128)(2,1)}, u32[]{:S(2)}, u32[]{:S(2)}) collective-permute-start(bf16[512,1024]{1,0:T(8,128)(2,1)} %shard_map.165.refs_7_.refs_1_), channel_id=1, source_target_pairs={{0,4},{4,0},{1,5},{5,1},{2,6},{6,2},{3,7},{7,3}} | collective-permute-start | bytes 3145736 | tf_op jit(solution)/shard_map/ppermute | solution.py:429
  936.8 86.7 %collective-permute-start.17 = (bf16[512,1024]{1,0:T(8,128)(2,1)}, bf16[512,1024]{1,0:T(8,128)(2,1)}, u32[]{:S(2)}, u32[]{:S(2)}) collective-permute-start(bf16[512,1024]{1,0:T(8,128)(2,1)} %shard_map.168.refs_7_.refs_1_), channel_id=1, source_target_pairs={{0,4},{4,0},{1,5},{5,1},{2,6},{6,2},{3,7},{7,3}} | collective-permute-start | bytes 3145736 | tf_op jit(solution)/shard_map/ppermute | solution.py:429
  946.4 72.7 %collective-permute-start.18 = (f32[256,2304]{1,0:T(8,128)}, f32[256,2304]{1,0:T(8,128)}, u32[]{:S(2)}, u32[]{:S(2)}) collective-permute-start(f32[256,2304]{1,0:T(8,128)} %get-tuple-element.98), channel_id=1, source_target_pairs={{0,4},{4,0},{1,5},{5,1},{2,6},{6,2},{3,7},{7,3}} | collective-permute-start | bytes 7077896 | tf_op jit(solution)/shard_map/ppermute | solution.py:429
  947.8 135.9 %collective-permute-start.21 = (f32[256,2304]{1,0:T(8,128)}, f32[256,2304]{1,0:T(8,128)}, u32[]{:S(2)}, u32[]{:S(2)}) collective-permute-start(f32[256,2304]{1,0:T(8,128)} %get-tuple-element.111), channel_id=1, source_target_pairs={{0,4},{4,0},{1,5},{5,1},{2,6},{6,2},{3,7},{7,3}} | collective-permute-start | bytes 7077896 | tf_op jit(solution)/shard_map/ppermute | solution.py:429
  1017.7 76.7 %collective-permute-start.24 = (f32[256,2304]{1,0:T(8,128)}, f32[256,2304]{1,0:T(8,128)}, u32[]{:S(2)}, u32[]{:S(2)}) collective-permute-start(f32[256,2304]{1,0:T(8,128)} %get-tuple-element.112), channel_id=1, source_target_pairs={{0,4},{4,0},{1,5},{5,1},{2,6},{6,2},{3,7},{7,3}} | collective-permute-start | bytes 7077896 | tf_op jit(solution)/shard_map/ppermute | solution.py:429
  1082.2 113.9 %collective-permute-start.20 = (f32[256,2304]{1,0:T(8,128)}, f32[256,2304]{1,0:T(8,128)}, u32[]{:S(2)}, u32[]{:S(2)}) collective-permute-start(f32[256,2304]{1,0:T(8,128)} %get-tuple-element.110), channel_id=1, source_target_pairs={{0,4},{4,0},{1,5},{5,1},{2,6},{6,2},{3,7},{7,3}} | collective-permute-start | bytes 7077896 | tf_op jit(solution)/shard_map/ppermute | solution.py:429
  1082.3 87.9 %collective-permute-start.23 = (bf16[256,2304]{1,0:T(8,128)(2,1)}, bf16[256,2304]{1,0:T(8,128)(2,1)}, u32[]{:S(2)}, u32[]{:S(2)}) collective-permute-start(bf16[256,2304]{1,0:T(8,128)(2,1)} %shard_map.171.refs_7_.refs_1_), channel_id=1, source_target_pairs={{0,4},{4,0},{1,5},{5,1},{2,6},{6,2},{3,7},{7,3}} | collective-permute-start | bytes 3538952 | tf_op jit(solution)/shard_map/ppermute | solution.py:429
  1087.9 105.0 %collective-permute-start.22 = (bf16[256,2304]{1,0:T(8,128)(2,1)}, bf16[256,2304]{1,0:T(8,128)(2,1)}, u32[]{:S(2)}, u32[]{:S(2)}) collective-permute-start(bf16[256,2304]{1,0:T(8,128)(2,1)} %shard_map.174.refs_4_.refs_1_), channel_id=1, source_target_pairs={{0,4},{4,0},{1,5},{5,1},{2,6},{6,2},{3,7},{7,3}} | collective-permute-start | bytes 3538952 | tf_op jit(solution)/shard_map/ppermute | solution.py:429
  1098.6 107.0 %collective-permute-start.26 = (bf16[256,2304]{1,0:T(8,128)(2,1)}, bf16[256,2304]{1,0:T(8,128)(2,1)}, u32[]{:S(2)}, u32[]{:S(2)}) collective-permute-start(bf16[256,2304]{1,0:T(8,128)(2,1)} %shard_map.175.refs_3_.refs_1_), channel_id=1, source_target_pairs={{0,4},{4,0},{1,5},{5,1},{2,6},{6,2},{3,7},{7,3}} | collective-permute-start | bytes 3538952 | tf_op jit(solution)/shard_map/ppermute | solution.py:429
  (15 other events, 359.8 us)
Sparse Core Ops, SparseCore 0:
  38.1 38.6 all-gather.6
  400.7 36.2 all-gather.12
  511.1 40.0 all-gather.8
  552.6 31.6 all-gather.14
  585.7 31.6 all-gather.10
  618.8 34.6 all-gather.16

commit v2 on v0

v2 whole, which is shorter than its diff:
```python
import functools

import jax
import jax.numpy as jnp
from jax import lax
from jax.experimental import pallas as pl
from jax.experimental.pallas import tpu as pltpu
from jax.sharding import PartitionSpec as P


THETAS = (10000.0, 1000000.0)
EPS = 1e-6
NEG_BIG = -1e30
LOG2E = 1.4426950408889634
F32 = jnp.float32
BF16 = jnp.bfloat16
VMEM_LIMIT = 67043328
ANY = pl.BlockSpec(memory_space=pl.ANY)


def rms_scale(values, gain):
    mean_sq = jnp.mean(values * values, axis=-1, keepdims=True)
    return values * lax.rsqrt(mean_sq + EPS) * (1.0 + gain)


def once(shape, index_map):
    return pl.BlockSpec(shape, index_map, pipeline_mode=pl.Buffered(1))


def run_kernel(kernel, args, in_specs, out_shape, out_specs, grid, scalars=(), deps=(), scratch=(), flops=0, nbytes=0, aliases=None):
    n_scalar = len(scalars)
    n_in = len(args)
    n_dep = len(deps)

    def body(*refs):
        head = refs[: n_scalar + n_in]
        tail = refs[n_scalar + n_in + n_dep:]
        kernel(*head, *tail)

    return pl.pallas_call(
        body,
        out_shape=out_shape,
        grid_spec=pltpu.PrefetchScalarGridSpec(
            num_scalar_prefetch=n_scalar,
            grid=grid,
            in_specs=list(in_specs) + [ANY] * n_dep,
            out_specs=out_specs,
            scratch_shapes=list(scratch),
        ),
        compiler_params=pltpu.CompilerParams(vmem_limit_bytes=VMEM_LIMIT, dimension_semantics=("arbitrary",) * len(grid)),
        cost_estimate=pl.CostEstimate(flops=int(flops), bytes_accessed=int(nbytes), transcendentals=0),
        input_output_aliases=aliases or {},
    )(*scalars, *args, *deps)


def copy_in(src, dst, sem):
    return pltpu.make_async_copy(src, dst, sem)


def sds(shape, dtype):
    return jax.ShapeDtypeStruct(shape, dtype)


def project_rows(x_rows, w_q, w_k, w_v, gain, qk_gain, base_tab, off_tab, q_out, kv_out, k_cache, v_cache, head_dim):
    normed = rms_scale(x_rows.astype(F32), gain).astype(BF16)
    rows = x_rows.shape[0]
    half = head_dim // 2
    cos_off, sin_off = off_tab[0], off_tab[1]
    cosines, sines = [], []
    for g in range(rows // 32):
        cos_base, sin_base = base_tab[0, g:g + 1, :], base_tab[1, g:g + 1, :]
        cosines.append(cos_base * cos_off - sin_base * sin_off)
        sines.append(sin_base * cos_off + cos_base * sin_off)
    cosine = jnp.concatenate(cosines, axis=0)
    sine_val = jnp.concatenate(sines, axis=0)

    def rotate(proj, head_gain):
        normed_head = rms_scale(proj, head_gain)
        lower, upper = normed_head[:, :half], normed_head[:, half:]
        return jnp.concatenate([lower * cosine - upper * sine_val, upper * cosine + lower * sine_val], axis=1).astype(BF16)

    n_kv = w_k.shape[-1] // head_dim
    kv_width = n_kv * head_dim
    for h in range(n_kv):
        cols = slice(h * head_dim, (h + 1) * head_dim)
        proj = jnp.dot(normed, w_k[:, cols], preferred_element_type=F32)
        kv_out[:, cols] = rotate(proj, qk_gain[1:2, :])
    for h in range(n_kv):
        cols = slice(h * head_dim, (h + 1) * head_dim)
        kv_out[:, kv_width + h * head_dim:kv_width + (h + 1) * head_dim] = jnp.dot(normed, w_v[:, cols], preferred_element_type=F32).astype(BF16)
    for h in range(w_q.shape[-1] // head_dim):
        cols = slice(h * head_dim, (h + 1) * head_dim)
        proj = jnp.dot(normed, w_q[:, cols], preferred_element_type=F32)
        q_out[:, cols] = rotate(proj, qk_gain[0:1, :])
    k_cache[...] = kv_out[:, :kv_width].reshape(rows, n_kv, head_dim)
    v_cache[...] = kv_out[:, kv_width:].reshape(rows, n_kv, head_dim)


def project(layer, tp_id, x_parts, row0, rows, weights, tabs, caches, total_rows, deps):
    w_q, w_k, w_v, norm_gain, qk_gain = weights
    base_tab, off_tab = tabs
    head_dim = qk_gain.shape[-1]
    paired = isinstance(x_parts, tuple)
    width = w_q.shape[1]
    bm = rows // 2 if paired else 256
    b0 = row0 // bm
    n_alias = 0 if caches is None else 2

    def block(i, tp):
        return lax.rem(i + tp[0], 2) if paired else i

    def kernel(tp, *refs):
        x_refs, refs = refs[:1 + paired], refs[1 + paired:]
        wq, wk, wv, ng, qg, bt, ot = refs[:7]
        outs = refs[7 + n_alias:]
        if paired:
            x_rows = jnp.where(pl.program_id(0) == 0, x_refs[0][...], x_refs[1][...])
            outs[4][...] = x_rows
        else:
            x_rows = x_refs[0][...]
        project_rows(x_rows, wq, wk, wv, ng[0:1, :], qg, bt, ot, *outs[:4], head_dim)

    nq, nkv = w_q.shape[-1], 2 * w_k.shape[-1]
    cache_shape = (2, total_rows, nkv // 2 // head_dim, head_dim)
    if paired:
        x_specs = [once((bm, width), lambda i, tp: (0, 0))] * 2
    else:
        x_specs = [pl.BlockSpec((bm, width), lambda i, tp: (b0 + i, 0))]
    cache_spec = pl.BlockSpec((None, bm) + cache_shape[2:], lambda i, tp: (layer, b0 + block(i, tp), 0, 0))
    in_specs = x_specs + [
        once((None,) + w_q.shape[1:], lambda i, tp: (layer, 0, 0)),
        once((None,) + w_k.shape[1:], lambda i, tp: (layer, 0, 0)),
        once((None,) + w_v.shape[1:], lambda i, tp: (layer, 0, 0)),
        once((None,) + norm_gain.shape[1:], lambda i, tp: (layer, 0, 0)),
        once((None,) + qk_gain.shape[1:], lambda i, tp: (layer, 0, 0)),
        pl.BlockSpec((None, 2, bm // 32, head_dim // 2), lambda i, tp: (layer, 0, b0 + block(i, tp), 0)),
        once((None, 2, 32, head_dim // 2), lambda i, tp: (layer, 0, 0, 0)),
    ] + [ANY] * n_alias
    out_shape = [sds((rows, nq), BF16), sds((rows, nkv), BF16), sds(cache_shape, BF16), sds(cache_shape, BF16)]
    out_specs = [pl.BlockSpec((bm, nq), lambda i, tp: (block(i, tp), 0)), pl.BlockSpec((bm, nkv), lambda i, tp: (block(i, tp), 0)), cache_spec, cache_spec]
    if paired:
        out_shape.append(sds((rows, width), BF16))
        out_specs.append(pl.BlockSpec((bm, width), lambda i, tp: (block(i, tp), 0)))
    args = (x_parts if paired else (x_parts,)) + tuple(weights) + (base_tab, off_tab) + (() if caches is None else tuple(caches))
    first_alias = 1 + len(args) - n_alias
    aliases = {first_alias + i: 2 + i for i in range(n_alias)}
    return run_kernel(
        kernel, args, in_specs, tuple(out_shape), out_specs, (rows // bm,), scalars=(tp_id,), deps=deps, aliases=aliases,
        flops=2 * rows * width * (nq + nkv), nbytes=2 * width * (nq + nkv + 2 * rows),
    )


def dot_t(a, b):
    return lax.dot_general(a, b, (((1,), (1,)), ((), ())), preferred_element_type=F32)


def causal(s):
    return jnp.where(lax.broadcasted_iota(jnp.int32, s.shape, 1) <= lax.broadcasted_iota(jnp.int32, s.shape, 0), s, NEG_BIG)


def windowed(s):
    return jnp.where(lax.broadcasted_iota(jnp.int32, s.shape, 1) > lax.broadcasted_iota(jnp.int32, s.shape, 0), s, NEG_BIG)


def row_max(scores):
    widest = max(s.shape[1] for s in scores)
    full = [s for s in scores if s.shape[1] == widest]
    tops = [jnp.max(functools.reduce(jnp.maximum, full), axis=1, keepdims=True)]
    tops += [jnp.max(s, axis=1, keepdims=True) for s in scores if s.shape[1] != widest]
    return functools.reduce(jnp.maximum, tops)


def row_sum(probs):
    widest = max(p.shape[1] for p in probs)
    full = [p for p in probs if p.shape[1] == widest]
    sums = [jnp.sum(functools.reduce(jnp.add, full), axis=1, keepdims=True)]
    sums += [jnp.sum(p, axis=1, keepdims=True) for p in probs if p.shape[1] != widest]
    return functools.reduce(jnp.add, sums)


def weighted(probs, values):
    return functools.reduce(jnp.add, [jnp.dot(p.astype(BF16), v, preferred_element_type=F32) for p, v in zip(probs, values)])


def local_attention(first, q, q_row, kv_blocks, head_dim, chunk, deps):
    nq = q.shape[1]
    nkv_heads = kv_blocks[0][0].shape[1] // (2 * head_dim)
    groups = nq // head_dim // nkv_heads
    factor = head_dim ** -0.5 * LOG2E
    sub = 256
    q_block = q_row // chunk

    def kernel(first_ref, q_ref, ka, va, kb, vb, kc, vc, o_ref):
        key_refs, val_refs = (ka, kb, kc), (va, vb, vc)
        units = [(g, r) for g in range(groups) for r in range(chunk // sub)]

        def pieces(r):
            out = []
            for b in range(3):
                for p in range(chunk // sub):
                    if b == 1 or (b == 0 and p > r) or (b == 2 and p < r):
                        out.append((b, p * sub, None))
                    elif p == r:
                        out.append((b, p * sub, windowed if b == 0 else causal))
            return out

        def scores_of(unit):
            g, r = unit
            q_rows = q_ref[r * sub:(r + 1) * sub, g * head_dim:(g + 1) * head_dim]
            scores = []
            for b, key0, mask in pieces(r):
                s = dot_t(q_rows, key_refs[b][key0:key0 + sub, :])
                if mask is not None:
                    s = mask(s)
                if kv_blocks[b][2]:
                    s = jnp.where(first_ref[0] == 1, NEG_BIG, s)
                scores.append(s)
            return scores

        scores = scores_of(units[0])
        for at, (g, r) in enumerate(units):
            later = scores_of(units[at + 1]) if at + 1 < len(units) else None
            top = row_max(scores)
            probs = [jnp.exp2((s - top) * factor) for s in scores]
            out = weighted(probs, [val_refs[b][key0:key0 + sub, :] for b, key0, _ in pieces(r)])
            o_ref[r * sub:(r + 1) * sub, g * head_dim:(g + 1) * head_dim] = (out / row_sum(probs)).astype(BF16)
            scores = later

    specs = [pl.BlockSpec((chunk, groups * head_dim), lambda i, f: (q_block, i))]
    args = [q]
    for array, block, _ in kv_blocks:
        specs.append(pl.BlockSpec((chunk, head_dim), lambda i, f, block=block: (block, i)))
        specs.append(pl.BlockSpec((chunk, head_dim), lambda i, f, block=block: (block, nkv_heads + i)))
        args += [array, array]
    return run_kernel(
        kernel, args, specs, sds((chunk, nq), BF16),
        pl.BlockSpec((chunk, groups * head_dim), lambda i, f: (0, i)), (nkv_heads,),
        scalars=(first,), deps=deps, flops=4 * chunk * 3 * chunk * nq, nbytes=10 * chunk * nq,
    )


def global_attention(rank, q, own, sources, head_dim, deps):
    chunk, nq = q.shape
    kv_width = own[0][1].shape[1]
    nkv_heads = kv_width // (2 * head_dim)
    groups = nq // head_dim // nkv_heads
    factor = head_dim ** -0.5 * LOG2E
    sub = 256
    n_part = chunk // sub
    units = [(g, r) for g in range(groups) for r in range(n_part)]
    q_start = own[-1][0]
    own_rows = q_start + chunk
    src_rows = sum(a.shape[0] for _, a in sources[0])
    piece = 512
    n_own, n_src = len(own), len(sources[0])

    def kernel(rank_ref, q_ref, *refs):
        own_refs, refs = refs[:n_own], refs[n_own:]
        src_refs, refs = [refs[i * n_src:(i + 1) * n_src] for i in range(3)], refs[3 * n_src:]
        o_ref, own_buf, src_buf, top_ref, total_ref, acc_ref, own_sems, src_sems = refs
        me = rank_ref[0]

        def own_copies():
            return [copy_in(ref, own_buf.at[row:row + ref.shape[0]], own_sems.at[i]) for i, (ref, (row, _)) in enumerate(zip(own_refs, own))]

        def src_copies(which, slot):
            return [copy_in(ref, src_buf.at[slot, row:row + ref.shape[0]], src_sems.at[slot, i]) for i, (ref, (row, _)) in enumerate(zip(src_refs[which], sources[0]))]

        def start_source(j):
            which = j + jnp.where(me == 2, 1, 0)
            slot = lax.rem(j, 2)
            for w in range(3):
                @pl.when(which == w)
                def _():
                    for copy in src_copies(w, slot):
                        copy.start()

        for copy in own_copies():
            copy.start()

        @pl.when(me > 0)
        def _():
            start_source(0)

        for copy in own_copies():
            copy.wait()

        def unit_refs(h, unit):
            g, r = unit
            rows = slice((g * n_part + r) * sub, (g * n_part + r + 1) * sub)
            q_rows = q_ref[r * sub:(r + 1) * sub, pl.ds(pl.multiple_of((h * groups + g) * head_dim, head_dim), head_dim)]
            return rows, q_rows

        def key_cols(h):
            return pl.ds(pl.multiple_of(h * head_dim, head_dim), head_dim)

        def val_cols(h):
            return pl.ds(pl.multiple_of((nkv_heads + h) * head_dim, head_dim), head_dim)

        @pl.loop(0, nkv_heads)
        def _(h):
            def bounds(r):
                limit = q_start + r * sub
                return [(i, min(i + piece, limit)) for i in range(0, limit, piece)] + [(limit, limit + sub)]

            def scores_of(unit):
                _, q_rows = unit_refs(h, unit)
                scores = [dot_t(q_rows, own_buf[lo:hi, key_cols(h)]) for lo, hi in bounds(unit[1])]
                return scores[:-1] + [causal(scores[-1])]

            scores = scores_of(units[0])
            for at, unit in enumerate(units):
                later = scores_of(units[at + 1]) if at + 1 < len(units) else None
                rows, _ = unit_refs(h, unit)
                top = row_max(scores)
                probs = [jnp.exp2((s - top) * factor) for s in scores]
                top_ref[h, rows, 0:1] = top
                total_ref[h, rows, 0:1] = row_sum(probs)
                acc_ref[h, rows, :] = weighted(probs, [own_buf[lo:hi, val_cols(h)] for lo, hi in bounds(unit[1])])
                scores = later

        @pl.loop(0, me)
        def _(j):
            slot = lax.rem(j, 2)
            for copy in src_copies(0, slot):
                copy.wait()

            @pl.when(j + 1 < me)
            def _():
                start_source(j + 1)

            @pl.loop(0, nkv_heads)
            def _(h):
                bounds = [(i, min(i + piece, src_rows)) for i in range(0, src_rows, piece)]

                def scores_of(unit):
                    _, q_rows = unit_refs(h, unit)
                    return [dot_t(q_rows, src_buf[slot, lo:hi, key_cols(h)]) for lo, hi in bounds]

                scores = scores_of(units[0])
                for at, unit in enumerate(units):
                    later = scores_of(units[at + 1]) if at + 1 < len(units) else None
                    rows, _ = unit_refs(h, unit)
                    old = top_ref[h, rows, 0:1]
                    top = jnp.maximum(old, row_max(scores))
                    alpha = jnp.exp2((old - top) * factor)
                    probs = [jnp.exp2((s - top) * factor) for s in scores]
                    top_ref[h, rows, 0:1] = top
                    total_ref[h, rows, 0:1] = total_ref[h, rows, 0:1] * alpha + row_sum(probs)
                    acc_ref[h, rows, :] = acc_ref[h, rows, :] * alpha + weighted(probs, [src_buf[slot, lo:hi, val_cols(h)] for lo, hi in bounds])
                    scores = later

        for h in range(nkv_heads):
            for g, r in units:
                rows = slice((g * n_part + r) * sub, (g * n_part + r + 1) * sub)
                o_ref[r * sub:(r + 1) * sub, (h * groups + g) * head_dim:(h * groups + g + 1) * head_dim] = (acc_ref[h, rows, :] / total_ref[h, rows, 0:1]).astype(BF16)

    args = [q] + [a for _, a in own] + [a for s in sources for _, a in s]
    return run_kernel(
        kernel, args, [pl.BlockSpec((chunk, nq), lambda i, f: (0, 0))] + [ANY] * (len(args) - 1),
        sds((chunk, nq), BF16), pl.BlockSpec((chunk, nq), lambda i, f: (0, 0)), (1,),
        scalars=(rank,), deps=deps,
        scratch=[pltpu.VMEM((own_rows, kv_width), BF16), pltpu.VMEM((2, src_rows, kv_width), BF16),
                 pltpu.VMEM((nkv_heads, groups * chunk, 128), F32), pltpu.VMEM((nkv_heads, groups * chunk, 128), F32),
                 pltpu.VMEM((nkv_heads, groups * chunk, head_dim), F32),
                 pltpu.SemaphoreType.DMA((n_own,)), pltpu.SemaphoreType.DMA((2, n_src))],
        flops=4 * chunk * (2 * src_rows) * nq, nbytes=16 * chunk * nq,
    )


def out_mlp(layer, ids, o_own, o_other, w_o, w_pieces, x, x_row, norm_gain, w_gate, w_up, w_down, deps):
    chunk, k_own = o_own.shape
    width = w_o.shape[-1]
    ff = w_gate.shape[-1]
    bm = chunk // 2
    bf = 512
    steps = ff // bf
    bk = 512
    n_k = k_own // bk
    quarter = w_pieces[0].shape[0]
    sub = 128

    def kernel(ids_ref, own_ref, oth_ref, wo_ref, p0, p1, p2, p3, x_ref, wg_ref, wu_ref, wd_ref, ng,
               send_ref, keep_ref, r_ref, o_buf, w_buf, x_buf, r_buf, m_buf, act_buf, acc_ref, g_buf, u_buf, d_buf, o_sems, w_sems, x_sem, t_sems, out_sems):
        tp, cp = ids_ref[0], ids_ref[1]
        halves = (1 - tp, tp)

        def rows_of(i, base=0):
            return pl.ds(pl.multiple_of(base + halves[i] * bm, bm), bm)

        own_w = [copy_in(wo_ref.at[layer, b * bk:(b + 1) * bk], w_buf.at[b * bk:(b + 1) * bk], w_sems.at[b]) for b in range(n_k)]
        oth_w = [copy_in(ref, w_buf.at[pl.ds(pl.multiple_of(k_own + quarter * lax.bitwise_xor(cp, flip), quarter), quarter)], w_sems.at[n_k + i])
                 for i, (ref, flip) in enumerate(((p0, 0), (p1, 2), (p2, 1), (p3, 3)))]
        o_copies = [[copy_in(ref.at[rows_of(i)], o_buf.at[i * bm:(i + 1) * bm, part * k_own:(part + 1) * k_own], o_sems.at[part, i]) for i in range(2)]
                    for part, ref in enumerate((own_ref, oth_ref))]
        x_copies = [copy_in(x_ref.at[rows_of(i, x_row)], x_buf.at[i * bm:(i + 1) * bm], x_sem.at[i]) for i in range(2)]

        def tile_copies(t, slot):
            cols = pl.ds(pl.multiple_of(t * bf, bf), bf)
            return (copy_in(wg_ref.at[layer, :, cols], g_buf.at[slot], t_sems.at[0, slot]),
                    copy_in(wu_ref.at[layer, :, cols], u_buf.at[slot], t_sems.at[1, slot]))

        def down_copy(t, slot):
            return copy_in(wd_ref.at[layer, pl.ds(pl.multiple_of(t * bf, bf), bf)], d_buf.at[slot], t_sems.at[2, slot])

        for copy in (*o_copies[0], own_w[0], own_w[1], *o_copies[1], *oth_w, *x_copies, *tile_copies(0, 0), down_copy(0, 0)):
            copy.start()

        for copy in o_copies[0]:
            copy.wait()
        for b in range(n_k):
            own_w[b].wait()
            part = jnp.dot(o_buf[:, b * bk:(b + 1) * bk], w_buf[b * bk:(b + 1) * bk, :], preferred_element_type=F32)
            acc_ref[...] = part if b == 0 else acc_ref[...] + part
        for copy in (*o_copies[1], *oth_w, *x_copies):
            copy.wait()
        other = jnp.dot(o_buf[:, k_own:], w_buf[k_own:, :], preferred_element_type=F32)
        acc_ref[...] = acc_ref[...] + other
        for row in range(0, chunk, sub):
            rows = slice(row, row + sub)
            resid = (x_buf[rows, :].astype(F32) + rms_scale(acc_ref[rows, :], ng[1:2, :])).astype(BF16)
            if row >= bm:
                r_buf[row - bm:row - bm + sub, :] = resid
            m_buf[rows, :] = rms_scale(resid.astype(F32), ng[2:3, :]).astype(BF16)
        r_copy = copy_in(r_buf, r_ref, out_sems.at[2])
        r_copy.start()

        def up_gate(slot):
            gate = jnp.dot(m_buf[...], g_buf[slot], preferred_element_type=F32)
            up = jnp.dot(m_buf[...], u_buf[slot], preferred_element_type=F32)
            return gate, up

        def activate(gate, up, slot):
            act_buf[slot] = (jax.nn.gelu(gate, approximate=True) * up).astype(BF16)

        for copy in tile_copies(0, 0):
            copy.wait()
        for copy in tile_copies(1, 1):
            copy.start()
        activate(*up_gate(0), 0)
        acc_ref[...] = jnp.zeros_like(acc_ref)

        @pl.loop(1, steps)
        def _(t):
            slot = lax.rem(t, 2)
            old = 1 - slot
            for copy in tile_copies(t, slot):
                copy.wait()
            down_copy(t - 1, old).wait()
            down_copy(t, slot).start()

            @pl.when(t + 1 < steps)
            def _():
                for copy in tile_copies(t + 1, old):
                    copy.start()

            gate, up = up_gate(slot)
            acc_ref[...] += jnp.dot(act_buf[old], d_buf[old], preferred_element_type=F32)
            activate(gate, up, slot)

        last = (steps - 1) % 2
        down_copy(steps - 1, last).wait()
        outs = []
        for i, ref in enumerate((send_ref, keep_ref)):
            rows = slice(i * bm, (i + 1) * bm)
            acc_ref[rows, :] += jnp.dot(act_buf[last, rows, :], d_buf[last], preferred_element_type=F32)
            outs.append(copy_in(acc_ref.at[rows], ref, out_sems.at[i]))
            outs[-1].start()
        for copy in outs:
            copy.wait()
        r_copy.wait()

    args = (o_own, o_other, w_o, *w_pieces, x, w_gate, w_up, w_down, norm_gain)
    return run_kernel(
        kernel, args, [ANY] * (len(args) - 1) + [pl.BlockSpec((None,) + norm_gain.shape[1:], lambda i, s: (layer, 0, 0))],
        (sds((bm, width), F32), sds((bm, width), F32), sds((bm, width), BF16)), [ANY] * 3, (1,), scalars=(ids,), deps=deps,
        scratch=[pltpu.VMEM((chunk, 2 * k_own), BF16), pltpu.VMEM((2 * k_own, width), BF16), pltpu.VMEM((chunk, width), BF16),
                 pltpu.VMEM((bm, width), BF16), pltpu.VMEM((chunk, width), BF16), pltpu.VMEM((2, chunk, bf), BF16), pltpu.VMEM((chunk, width), F32),
                 pltpu.VMEM((2, width, bf), BF16), pltpu.VMEM((2, width, bf), BF16), pltpu.VMEM((2, bf, width), BF16),
                 pltpu.SemaphoreType.DMA((2, 2)), pltpu.SemaphoreType.DMA((n_k + 4,)), pltpu.SemaphoreType.DMA((2,)),
                 pltpu.SemaphoreType.DMA((3, 2)), pltpu.SemaphoreType.DMA((3,))],
        flops=4 * chunk * k_own * width + 6 * chunk * width * ff, nbytes=6 * width * ff + 4 * k_own * width + 20 * chunk * width,
    )


def finish_rows(layer, kept, received, r, norm_gain, deps):
    rows, width = kept.shape
    bm = 64

    def kernel(kept_ref, recv_ref, r_ref, ng, x_ref):
        x_ref[...] = (r_ref[...].astype(F32) + rms_scale(kept_ref[...] + recv_ref[...], ng[3:4, :])).astype(BF16)

    row_spec = pl.BlockSpec((bm, width), lambda i: (i, 0))
    return run_kernel(
        kernel, (kept, received, r, norm_gain),
        [row_spec, row_spec, row_spec, once((None,) + norm_gain.shape[1:], lambda i: (layer, 0, 0))],
        sds((rows, width), BF16), row_spec, (rows // bm,), deps=deps, flops=20 * rows * width, nbytes=12 * rows * width,
    )


def place_rows(tp_id, x_keep, x_other, row0, total_rows, target, deps):
    bm, width = x_keep.shape
    b0 = row0 // bm

    def half(i, tp):
        return lax.rem(i + tp[0], 2)

    def kernel(tp, keep_ref, other_ref, *refs):
        refs[-1][...] = jnp.where(pl.program_id(0) == 0, keep_ref[...], other_ref[...])

    specs = [once((bm, width), lambda i, tp: (0, 0)), once((bm, width), lambda i, tp: (0, 0))]
    args = [x_keep, x_other]
    aliases = None
    if target is not None:
        specs.append(ANY)
        args.append(target)
        aliases = {3: 0}
    return run_kernel(
        kernel, args, specs, sds((total_rows, width), BF16),
        pl.BlockSpec((bm, width), lambda i, tp: (b0 + half(i, tp), 0)), (2,), scalars=(tp_id,), deps=deps, aliases=aliases,
        flops=bm * width, nbytes=8 * bm * width,
    )


CHUNKS = ((0, 512), (512, 512), (1024, 512), (1536, 512))
SEQUENCE = (
    ("swap", 0, 0), ("qkv", 0, 1), ("halo", 0, 0), ("qkv", 0, 0), ("swapx", 0, 0), ("attn", 0, 2), ("attn", 0, 3), ("attn", 0, 0), ("attn", 0, 1),
    ("swapd", 0, 0), ("wm", 0, 2), ("wm", 0, 3), ("wm", 0, 0), ("post", 0, 2), ("wm", 0, 1), ("post", 0, 3), ("post", 0, 0),
    ("qkv", 1, 2), ("post", 0, 1), ("swap", 1, 0), ("qkv", 1, 3), ("fwd", 1, 2), ("qkv", 1, 0), ("fwd", 1, 3), ("qkv", 1, 1),
    ("fwd", 1, 0), ("swapx", 1, 0), ("fwd", 1, 1),
    ("attn", 1, 2), ("attn", 1, 3), ("swapd", 1, 0), ("wm", 1, 2), ("attn", 1, 0), ("wm", 1, 3), ("attn", 1, 1), ("wm", 1, 0), ("post", 1, 2),
    ("wm", 1, 1), ("post", 1, 3), ("post", 1, 0), ("place", 1, 2), ("place", 1, 3), ("post", 1, 1), ("place", 1, 0), ("place", 1, 1),
)


def solution(mesh):
    assert mesh.shape['cp'] == 4 and mesh.shape['tp'] == 2
    row_spec = P(('dp', 'cp'), None)
    col_spec = P(None, None, 'tp')
    row_w_spec = P(None, 'tp', None)
    cache_spec = P(None, ('dp', 'cp'), 'tp', None)
    swap_tp = [(0, 1), (1, 0)]
    swap_core = [(0, 1), (1, 0), (2, 3), (3, 2)]
    swap_chip = [(0, 2), (2, 0), (1, 3), (3, 1)]

    def device_fn(hidden, positions, w_q, w_k, w_v, w_o, w_gate, w_up, w_down, norm_gain, qk_gain):
        tok_rows, width = hidden.shape
        head_dim = qk_gain.shape[-1]
        half_dim = head_dim // 2
        high = tok_rows // 2
        tp_index = lax.axis_index('tp').astype(jnp.int32)
        cp_index = lax.axis_index('cp').astype(jnp.int32)
        tp_id, rank = tp_index.reshape(1), cp_index.reshape(1)
        ids = jnp.stack([tp_index, cp_index])
        first = (cp_index == 0).astype(jnp.int32).reshape(1)

        def permute(value, axis, pairs):
            return lax.ppermute(value, axis, pairs)

        def tied(value):
            return lax.optimization_barrier((value, deps[0]))[0] if deps else value

        theta_col = jnp.array(THETAS, F32)[:, None]
        inv_freq = theta_col ** (-(jnp.arange(half_dim, dtype=F32) * 2.0) / head_dim)[None, :]
        base_pos = (positions[0] + 32 * jnp.arange(tok_rows // 32, dtype=jnp.int32)).astype(F32)
        base_ang = base_pos[None, :, None] * inv_freq[:, None, :]
        off_ang = jnp.arange(32, dtype=F32)[None, :, None] * inv_freq[:, None, :]
        tabs = (jnp.stack([jnp.cos(base_ang), jnp.sin(base_ang)], axis=1), jnp.stack([jnp.cos(off_ang), jnp.sin(off_ang)], axis=1))

        quarter = w_o.shape[1] // 4
        weights = (w_q, w_k, w_v, norm_gain, qk_gain)
        w_pieces, q_rot, kv_own, kv_d, kv_x, kv_f, x_mid = {}, {}, {}, {}, {}, {}, {}
        o_own, o_oth, r_rows, kept, recv, x_keep, x_oth = {}, {}, {}, {}, {}, {}, {}
        halo = out = caches = None
        deps = ()

        for kind, layer, c in SEQUENCE:
            row, rows = (c * high, high) if kind == "qkv" and layer == 0 else CHUNKS[c]
            result = None
            if kind == "swap":
                piece = lax.dynamic_slice(w_o, (layer, cp_index * quarter, 0), (1, quarter, width))[0]
                w_pieces[layer] = [permute(tied(piece), 'tp', swap_tp)]
            elif kind == "swapx":
                w_pieces[layer].append(permute(tied(w_pieces[layer][0]), 'cp', swap_chip))
            elif kind == "swapd":
                w_pieces[layer] += [permute(tied(w_pieces[layer][0]), 'cp', swap_core), permute(tied(w_pieces[layer][1]), 'cp', swap_core)]
            elif kind == "halo":
                halo = permute(kv_own[0, 1], 'cp', [(i, i + 1) for i in range(3)])
            elif kind == "qkv" and layer == 0:
                q_rot[0, c], kv_own[0, c], *caches = project(0, tp_id, hidden, row, rows, weights, tabs, caches, tok_rows, deps)
                result = q_rot[0, c]
            elif kind == "qkv":
                q_rot[1, c], kv_own[1, c], *caches, x_mid[c] = project(1, tp_id, (x_keep[0, c], x_oth[0, c]), row, rows, weights, tabs, caches, tok_rows, deps)
                result = q_rot[1, c]
                kv_d[c] = permute(kv_own[1, c], 'cp', swap_core)
                kv_x[c] = permute(kv_own[1, c], 'cp', swap_chip)
            elif kind == "fwd":
                kv_f[c] = permute(tied(kv_x[c]), 'cp', swap_core)
            elif kind == "attn" and layer == 0:
                blocks = []
                for start in (row - 2 * rows, row - rows, row):
                    array = halo if start < 0 else kv_own[0, start // high]
                    blocks.append((array, start % high // rows, start < 0))
                result = o_own[c] = local_attention(first, q_rot[0, row // high], row % high, blocks, head_dim, rows, deps)
            elif kind == "attn":
                own = [(start, kv_own[1, i]) for i, (start, _) in enumerate(CHUNKS) if start <= row]
                sources = [[(CHUNKS[i][0], held[i]) for i in range(len(CHUNKS))] for held in (kv_d, kv_x, kv_f)]
                result = o_own[c] = global_attention(rank, q_rot[1, c], own, sources, head_dim, deps)
            elif kind == "wm":
                x, x_row = (hidden, row) if layer == 0 else (x_mid[c], 0)
                send, kept[c], r_rows[c] = out_mlp(layer, ids, o_own[c], o_oth[c], w_o, w_pieces[layer], x, x_row, norm_gain, w_gate, w_up, w_down, deps)
                recv[c] = permute(send, 'tp', swap_tp)
                result = kept[c]
            elif kind == "post":
                result = x_keep[layer, c] = finish_rows(layer, kept[c], recv[c], r_rows[c], norm_gain, deps)
                x_oth[layer, c] = permute(result, 'tp', swap_tp)
            elif kind == "place":
                result = out = place_rows(tp_id, x_keep[1, c], x_oth[1, c], row, tok_rows, out, deps if out is None or deps[0] is not out else ())
            if kind == "attn":
                o_oth[c] = permute(result, 'tp', swap_tp)
            if result is not None:
                deps = (result,)
        return out, caches[0], caches[1]

    return jax.shard_map(
        device_fn,
        mesh=mesh,
        in_specs=(row_spec, P(('dp', 'cp')), col_spec, col_spec, col_spec, row_w_spec, col_spec, col_spec, row_w_spec, P(), P()),
        out_specs=(row_spec, cache_spec, cache_spec),
        check_vma=False,
    )
```

time: 3100 us -> 1050 us (0.34)
  the two profiles are of different devices: /device:TPU:0 before, /device:TPU:3 now
where the time goes in v2:
time: 1050 us
  Pallas kernels  682 us (65%)
  waiting for transfers between devices  315 us (30%)
  starting transfers between devices  38.9 us (4%)
    pallas_call x34, Pallas kernels, run_kernel(): pl.pallas_call(body, out_shape=out_shape, grid_spec=pltpu.PrefetchScalarG...  682 us
    ppermute x45, waiting for transfers between devices, permute(): return lax.ppermute(value, axis, pairs)  315 us
    ppermute x45, starting transfers between devices, permute(): return lax.ppermute(value, axis, pairs)  38.9 us
  transfers between devices with their start and end apart: 45, of which 17 were waited for; matrix products, arithmetic and copies ran while one was open for 0% of the time, Pallas kernels for 63%

profile of v2, /device:TPU:3, one launch (start us, length us, event | category | flops | bytes accessed | tf_op | source)
XLA Modules:
  0.0 1046.8 jit_solution(11143187067439406831)
XLA Ops:
  5.0 18.8 %shard_map.139 = (bf16[1024,1024]{1,0:T(8,128)(2,1)}, bf16[1024,1024]{1,0:T(8,128)(2,1)}, bf16[2,2048,2,256]{3,2,1,0:T(2,128)(2,1)}, bf16[2,2048,2,256]{3,2,1,0:T(2,128)(2,1)}) custom-call(s32[1]{0:T(128)} %bitcast.refs_0_, bf16[2048,2304]{1,0:T(8,128)(2,1)} %refs_8_.7, bf16[2,2304,1024]{2,1,0:T(8,128)(2,1)} %refs_3_.35, bf16[2,2304,512]{2,1,0:T(8,128)(2,1)} %refs_4_.11, ...), custom_call_target="tpu_custom_call" | custom-call | flops 9663676416 | bytes 18874368 | tf_op jit(solution)/shard_map/pallas_call | solution.py:40
  30.1 18.8 %shard_map.140 = (bf16[1024,1024]{1,0:T(8,128)(2,1)}, bf16[1024,1024]{1,0:T(8,128)(2,1)}, bf16[2,2048,2,256]{3,2,1,0:T(2,128)(2,1)}, bf16[2,2048,2,256]{3,2,1,0:T(2,128)(2,1)}) custom-call(s32[1]{0:T(128)} %bitcast.refs_0_, bf16[2048,2304]{1,0:T(8,128)(2,1)} %refs_8_.7, ...), custom_call_target="tpu_custom_call", output_to_operand_aliasing={{2}: (9, {}), {3}: (10, {})} | custom-call | flops 9663676416 | bytes 18874368 | tf_op jit(solution)/shard_map/pallas_call | solution.py:40
  91.6 21.3 %collective-permute-done.6.refs_2_ = bf16[512,1024]{1,0:T(8,128)(2,1)} collective-permute-done((bf16[512,1024]{1,0:T(8,128)(2,1)}, bf16[512,1024]{1,0:T(8,128)(2,1)}, u32[]{:S(2)}, u32[]{:S(2)}) %collective-permute-start.6) | collective-permute-done | bytes 1048608 | tf_op jit(solution)/shard_map/ppermute | solution.py:558
  114.1 49.5 %shard_map.145 = (f32[256,2304]{1,0:T(8,128)}, f32[256,2304]{1,0:T(8,128)}, bf16[256,2304]{1,0:T(8,128)(2,1)}) custom-call(s32[2]{0:T(128)} %pad_add_fusion.refs_0_, bf16[512,1024]{1,0:T(8,128)(2,1)} %shard_map.141.refs_8_.refs_1_, bf16[512,1024]{1,0:T(8,128)(2,1)} %collective-permute-done.6.refs_2_, bf16[2,1024,2304]{2,1,0:T(8,128)(2,1)} %refs_3_.40, ...), custom_call_target="tpu_custom_call" | custom-call | flops 37446746112 | bytes 96731136 | tf_op jit(solution)/shard_map/pallas_call | solution.py:40
  163.8 49.8 %shard_map.146 = (f32[256,2304]{1,0:T(8,128)}, f32[256,2304]{1,0:T(8,128)}, bf16[256,2304]{1,0:T(8,128)(2,1)}) custom-call(s32[2]{0:T(128)} %pad_add_fusion.refs_0_, bf16[512,1024]{1,0:T(8,128)(2,1)} %shard_map.142.refs_8_.refs_1_, bf16[512,1024]{1,0:T(8,128)(2,1)} %collective-permute-done.9.refs_2_, bf16[2,1024,2304]{2,1,0:T(8,128)(2,1)} %refs_3_.40, ...), custom_call_target="tpu_custom_call" | custom-call | flops 37446746112 | bytes 96731136 | tf_op jit(solution)/shard_map/pallas_call | solution.py:40
  214.9 50.0 %shard_map.147 = (f32[256,2304]{1,0:T(8,128)}, f32[256,2304]{1,0:T(8,128)}, bf16[256,2304]{1,0:T(8,128)(2,1)}) custom-call(s32[2]{0:T(128)} %pad_add_fusion.refs_0_, bf16[512,1024]{1,0:T(8,128)(2,1)} %shard_map.143.refs_8_.refs_1_, bf16[512,1024]{1,0:T(8,128)(2,1)} %collective-permute-done.8.refs_2_, bf16[2,1024,2304]{2,1,0:T(8,128)(2,1)} %refs_3_.40, ...), custom_call_target="tpu_custom_call" | custom-call | flops 37446746112 | bytes 96731136 | tf_op jit(solution)/shard_map/pallas_call | solution.py:40
  270.1 49.6 %shard_map.149 = (f32[256,2304]{1,0:T(8,128)}, f32[256,2304]{1,0:T(8,128)}, bf16[256,2304]{1,0:T(8,128)(2,1)}) custom-call(s32[2]{0:T(128)} %pad_add_fusion.refs_0_, bf16[512,1024]{1,0:T(8,128)(2,1)} %shard_map.144.refs_13_.refs_1_, bf16[512,1024]{1,0:T(8,128)(2,1)} %collective-permute-done.1.refs_2_, bf16[2,1024,2304]{2,1,0:T(8,128)(2,1)} %refs_3_.40, ...), custom_call_target="tpu_custom_call" | custom-call | flops 37446746112 | bytes 96731136 | tf_op jit(solution)/shard_map/pallas_call | solution.py:40
  338.1 69.7 %collective-permute-done.11.refs_2_ = bf16[256,2304]{1,0:T(8,128)(2,1)} collective-permute-done((bf16[256,2304]{1,0:T(8,128)(2,1)}, bf16[256,2304]{1,0:T(8,128)(2,1)}, u32[]{:S(2)}, u32[]{:S(2)}) %collective-permute-start.11) | collective-permute-done | bytes 1179680 | tf_op jit(solution)/shard_map/ppermute | solution.py:558
  433.1 12.4 %shard_map.154 = (bf16[512,1024]{1,0:T(8,128)(2,1)}, bf16[512,1024]{1,0:T(8,128)(2,1)}, bf16[2,2048,2,256]{3,2,1,0:T(2,128)(2,1)}, bf16[2,2048,2,256]{3,2,1,0:T(2,128)(2,1)}, bf16[512,2304]{1,0:T(8,128)(2,1)}) custom-call(s32[1]{0:T(128)} %bitcast.refs_0_, ...), custom_call_target="tpu_custom_call", output_to_operand_aliasing={{2}: (10, {}), {3}: (11, {})} | custom-call | flops 4831838208 | bytes 14155776 | tf_op jit(solution)/shard_map/pallas_call | solution.py:40
  483.7 12.6 %shard_map.156 = (bf16[512,1024]{1,0:T(8,128)(2,1)}, bf16[512,1024]{1,0:T(8,128)(2,1)}, bf16[2,2048,2,256]{3,2,1,0:T(2,128)(2,1)}, bf16[2,2048,2,256]{3,2,1,0:T(2,128)(2,1)}, bf16[512,2304]{1,0:T(8,128)(2,1)}) custom-call(s32[1]{0:T(128)} %bitcast.refs_0_, ...), custom_call_target="tpu_custom_call", output_to_operand_aliasing={{2}: (10, {}), {3}: (11, {})} | custom-call | flops 4831838208 | bytes 14155776 | tf_op jit(solution)/shard_map/pallas_call | solution.py:40
  499.1 19.8 %collective-permute-done.22.refs_10_.refs_11_.refs_8_.refs_9_ = bf16[512,1024]{1,0:T(8,128)(2,1)S(1)} collective-permute-done((bf16[512,1024]{1,0:T(8,128)(2,1)}, bf16[512,1024]{1,0:T(8,128)(2,1)S(1)}, u32[]{:S(2)}, u32[]{:S(2)}) %collective-permute-start.22) | collective-permute-done | bytes 1048608 | tf_op jit(solution)/shard_map/ppermute | solution.py:558
  531.1 30.8 %shard_map.157.refs_18_.refs_1_ = bf16[512,1024]{1,0:T(8,128)(2,1)} custom-call(s32[1]{0:T(128)} %bitcast.1.refs_0_, bf16[512,1024]{1,0:T(8,128)(2,1)} %get-tuple-element.89.refs_4_.refs_1_, bf16[512,1024]{1,0:T(8,128)(2,1)} %get-tuple-element.99.refs_2_, bf16[512,1024]{1,0:T(8,128)(2,1)} %get-tuple-element.100.refs_3_, ...), custom_call_target="tpu_custom_call" | custom-call | flops 8589934592 | bytes 8388608 | tf_op jit(solution)/shard_map/pallas_call | solution.py:40
  561.9 33.2 %shard_map.158.refs_13_.refs_1_ = bf16[512,1024]{1,0:T(8,128)(2,1)} custom-call(s32[1]{0:T(128)} %bitcast.1.refs_0_, bf16[512,1024]{1,0:T(8,128)(2,1)} %get-tuple-element.94.refs_12_.refs_1_, bf16[512,1024]{1,0:T(8,128)(2,1)} %get-tuple-element.99.refs_2_, bf16[512,1024]{1,0:T(8,128)(2,1)} %get-tuple-element.100.refs_3_, ...), custom_call_target="tpu_custom_call" | custom-call | flops 8589934592 | bytes 8388608 | tf_op jit(solution)/shard_map/pallas_call | solution.py:40
  597.1 23.5 %collective-permute-done.34.refs_2_ = bf16[512,1024]{1,0:T(8,128)(2,1)} collective-permute-done((bf16[512,1024]{1,0:T(8,128)(2,1)}, bf16[512,1024]{1,0:T(8,128)(2,1)}, u32[]{:S(2)}, u32[]{:S(2)}) %collective-permute-start.34) | collective-permute-done | bytes 1048608 | tf_op jit(solution)/shard_map/ppermute | solution.py:558
  620.7 49.6 %shard_map.159 = (f32[256,2304]{1,0:T(8,128)}, f32[256,2304]{1,0:T(8,128)}, bf16[256,2304]{1,0:T(8,128)(2,1)}) custom-call(s32[2]{0:T(128)} %pad_add_fusion.refs_0_, bf16[512,1024]{1,0:T(8,128)(2,1)} %shard_map.157.refs_18_.refs_1_, bf16[512,1024]{1,0:T(8,128)(2,1)} %collective-permute-done.34.refs_2_, bf16[2,1024,2304]{2,1,0:T(8,128)(2,1)} %refs_3_.40, ...), custom_call_target="tpu_custom_call" | custom-call | flops 37446746112 | bytes 96731136 | tf_op jit(solution)/shard_map/pallas_call | solution.py:40
  670.3 26.0 %shard_map.160.refs_13_.refs_1_ = bf16[512,1024]{1,0:T(8,128)(2,1)} custom-call(s32[1]{0:T(128)} %bitcast.1.refs_0_, bf16[512,1024]{1,0:T(8,128)(2,1)} %get-tuple-element.97.refs_12_.refs_1_, bf16[512,1024]{1,0:T(8,128)(2,1)} %get-tuple-element.99.refs_2_, bf16[512,1024]{1,0:T(8,128)(2,1)} %copy-done.3, bf16[512,1024]{1,0:T(8,128)(2,1)} %copy-done.6, ...), custom_call_target="tpu_custom_call" | custom-call | flops 8589934592 | bytes 8388608 | tf_op jit(solution)/shard_map/pallas_call | solution.py:40
  697.8 49.3 %shard_map.161 = (f32[256,2304]{1,0:T(8,128)}, f32[256,2304]{1,0:T(8,128)}, bf16[256,2304]{1,0:T(8,128)(2,1)}) custom-call(s32[2]{0:T(128)} %pad_add_fusion.refs_0_, bf16[512,1024]{1,0:T(8,128)(2,1)} %shard_map.158.refs_13_.refs_1_, bf16[512,1024]{1,0:T(8,128)(2,1)} %collective-permute-done.29.refs_2_, bf16[2,1024,2304]{2,1,0:T(8,128)(2,1)} %refs_3_.40, ...), custom_call_target="tpu_custom_call" | custom-call | flops 37446746112 | bytes 96731136 | tf_op jit(solution)/shard_map/pallas_call | solution.py:40
  747.1 29.5 %shard_map.162.refs_13_.refs_1_ = bf16[512,1024]{1,0:T(8,128)(2,1)} custom-call(s32[1]{0:T(128)} %bitcast.1.refs_0_, bf16[512,1024]{1,0:T(8,128)(2,1)} %get-tuple-element.98.refs_17_.refs_1_, bf16[512,1024]{1,0:T(8,128)(2,1)} %get-tuple-element.99.refs_2_, bf16[512,1024]{1,0:T(8,128)(2,1)} %get-tuple-element.100.refs_3_, bf16[512,1024]{1,0:T(8,128)(2,1)} %copy-done.3, ...), custom_call_target="tpu_custom_call" | custom-call | flops 8589934592 | bytes 8388608 | tf_op jit(solution)/shard_map/pallas_call | solution.py:40
  778.1 49.2 %shard_map.163 = (f32[256,2304]{1,0:T(8,128)}, f32[256,2304]{1,0:T(8,128)}, bf16[256,2304]{1,0:T(8,128)(2,1)}) custom-call(s32[2]{0:T(128)} %pad_add_fusion.refs_0_, bf16[512,1024]{1,0:T(8,128)(2,1)} %shard_map.160.refs_13_.refs_1_, bf16[512,1024]{1,0:T(8,128)(2,1)} %collective-permute-done.37.refs_2_, bf16[2,1024,2304]{2,1,0:T(8,128)(2,1)} %refs_3_.40, ...), custom_call_target="tpu_custom_call" | custom-call | flops 37446746112 | bytes 96731136 | tf_op jit(solution)/shard_map/pallas_call | solution.py:40
  833.4 49.5 %shard_map.165 = (f32[256,2304]{1,0:T(8,128)}, f32[256,2304]{1,0:T(8,128)}, bf16[256,2304]{1,0:T(8,128)(2,1)}) custom-call(s32[2]{0:T(128)} %pad_add_fusion.refs_0_, bf16[512,1024]{1,0:T(8,128)(2,1)} %shard_map.162.refs_13_.refs_1_, bf16[512,1024]{1,0:T(8,128)(2,1)} %collective-permute-done.35.refs_2_, bf16[2,1024,2304]{2,1,0:T(8,128)(2,1)} %refs_3_.40, ...), custom_call_target="tpu_custom_call" | custom-call | flops 37446746112 | bytes 96731136 | tf_op jit(solution)/shard_map/pallas_call | solution.py:40
  889.3 14.0 %collective-permute-done.42.refs_1_ = f32[256,2304]{1,0:T(8,128)} collective-permute-done((f32[256,2304]{1,0:T(8,128)}, f32[256,2304]{1,0:T(8,128)}, u32[]{:S(2)}, u32[]{:S(2)}) %collective-permute-start.42) | collective-permute-done | bytes 2359328 | tf_op jit(solution)/shard_map/ppermute | solution.py:558
  909.2 69.9 %collective-permute-done.41.refs_2_ = bf16[256,2304]{1,0:T(8,128)(2,1)} collective-permute-done((bf16[256,2304]{1,0:T(8,128)(2,1)}, bf16[256,2304]{1,0:T(8,128)(2,1)}, u32[]{:S(2)}, u32[]{:S(2)}) %collective-permute-start.41) | collective-permute-done | bytes 1179680 | tf_op jit(solution)/shard_map/ppermute | solution.py:558
  982.3 22.1 %collective-permute-done.40.refs_2_ = bf16[256,2304]{1,0:T(8,128)(2,1)} collective-permute-done((bf16[256,2304]{1,0:T(8,128)(2,1)}, bf16[256,2304]{1,0:T(8,128)(2,1)}, u32[]{:S(2)}, u32[]{:S(2)}) %collective-permute-start.40) | collective-permute-done | bytes 1179680 | tf_op jit(solution)/shard_map/ppermute | solution.py:558
  1013.5 16.2 %collective-permute-done.44.refs_2_ = bf16[256,2304]{1,0:T(8,128)(2,1)} collective-permute-done((bf16[256,2304]{1,0:T(8,128)(2,1)}, bf16[256,2304]{1,0:T(8,128)(2,1)}, u32[]{:S(2)}, u32[]{:S(2)}) %collective-permute-start.44) | collective-permute-done | bytes 1179680 | tf_op jit(solution)/shard_map/ppermute | solution.py:558
  (126 shorter events, 210.7 us)
Async XLA Ops:
  89.6 74.3 %collective-permute-start.9 = (bf16[512,1024]{1,0:T(8,128)(2,1)}, bf16[512,1024]{1,0:T(8,128)(2,1)}, u32[]{:S(2)}, u32[]{:S(2)}) collective-permute-start(bf16[512,1024]{1,0:T(8,128)(2,1)} %shard_map.142.refs_8_.refs_1_), channel_id=1, source_target_pairs={{0,4},{4,0},{1,5},{5,1},{2,6},{6,2},{3,7},{7,3}} | collective-permute-start | bytes 3145736 | tf_op jit(solution)/shard_map/ppermute | solution.py:558
  90.4 124.5 %collective-permute-start.8 = (bf16[512,1024]{1,0:T(8,128)(2,1)}, bf16[512,1024]{1,0:T(8,128)(2,1)}, u32[]{:S(2)}, u32[]{:S(2)}) collective-permute-start(bf16[512,1024]{1,0:T(8,128)(2,1)} %shard_map.143.refs_8_.refs_1_), channel_id=1, source_target_pairs={{0,4},{4,0},{1,5},{5,1},{2,6},{6,2},{3,7},{7,3}} | collective-permute-start | bytes 3145736 | tf_op jit(solution)/shard_map/ppermute | solution.py:558
  112.9 157.2 %collective-permute-start.1 = (bf16[512,1024]{1,0:T(8,128)(2,1)}, bf16[512,1024]{1,0:T(8,128)(2,1)}, u32[]{:S(2)}, u32[]{:S(2)}) collective-permute-start(bf16[512,1024]{1,0:T(8,128)(2,1)} %shard_map.144.refs_13_.refs_1_), channel_id=1, source_target_pairs={{0,4},{4,0},{1,5},{5,1},{2,6},{6,2},{3,7},{7,3}} | collective-permute-start | bytes 3145736 | tf_op jit(solution)/shard_map/ppermute | solution.py:558
  163.6 101.6 %collective-permute-start.7 = (f32[256,2304]{1,0:T(8,128)}, f32[256,2304]{1,0:T(8,128)}, u32[]{:S(2)}, u32[]{:S(2)}) collective-permute-start(f32[256,2304]{1,0:T(8,128)} %get-tuple-element.76), channel_id=1, source_target_pairs={{0,4},{4,0},{1,5},{5,1},{2,6},{6,2},{3,7},{7,3}} | collective-permute-start | bytes 7077896 | tf_op jit(solution)/shard_map/ppermute | solution.py:558
  213.7 107.5 %collective-permute-start.13 = (f32[256,2304]{1,0:T(8,128)}, f32[256,2304]{1,0:T(8,128)}, u32[]{:S(2)}, u32[]{:S(2)}) collective-permute-start(f32[256,2304]{1,0:T(8,128)} %get-tuple-element.87), channel_id=1, source_target_pairs={{0,4},{4,0},{1,5},{5,1},{2,6},{6,2},{3,7},{7,3}} | collective-permute-start | bytes 7077896 | tf_op jit(solution)/shard_map/ppermute | solution.py:558
  264.9 67.0 %collective-permute-start.12 = (f32[256,2304]{1,0:T(8,128)}, f32[256,2304]{1,0:T(8,128)}, u32[]{:S(2)}, u32[]{:S(2)}) collective-permute-start(f32[256,2304]{1,0:T(8,128)} %get-tuple-element.85), channel_id=1, source_target_pairs={{0,4},{4,0},{1,5},{5,1},{2,6},{6,2},{3,7},{7,3}} | collective-permute-start | bytes 7077896 | tf_op jit(solution)/shard_map/ppermute | solution.py:558
  319.7 101.1 %collective-permute-start.10 = (f32[256,2304]{1,0:T(8,128)}, f32[256,2304]{1,0:T(8,128)}, u32[]{:S(2)}, u32[]{:S(2)}) collective-permute-start(f32[256,2304]{1,0:T(8,128)} %get-tuple-element.81), channel_id=1, source_target_pairs={{0,4},{4,0},{1,5},{5,1},{2,6},{6,2},{3,7},{7,3}} | collective-permute-start | bytes 7077896 | tf_op jit(solution)/shard_map/ppermute | solution.py:558
  320.9 86.9 %collective-permute-start.11 = (bf16[256,2304]{1,0:T(8,128)(2,1)}, bf16[256,2304]{1,0:T(8,128)(2,1)}, u32[]{:S(2)}, u32[]{:S(2)}) collective-permute-start(bf16[256,2304]{1,0:T(8,128)(2,1)} %shard_map.148.refs_13_.refs_1_), channel_id=1, source_target_pairs={{0,4},{4,0},{1,5},{5,1},{2,6},{6,2},{3,7},{7,3}} | collective-permute-start | bytes 3538952 | tf_op jit(solution)/shard_map/ppermute | solution.py:558
  326.2 106.9 %collective-permute-start.16 = (bf16[256,2304]{1,0:T(8,128)(2,1)}, bf16[256,2304]{1,0:T(8,128)(2,1)}, u32[]{:S(2)}, u32[]{:S(2)}) collective-permute-start(bf16[256,2304]{1,0:T(8,128)(2,1)} %shard_map.150.refs_4_.refs_1_), channel_id=1, source_target_pairs={{0,4},{4,0},{1,5},{5,1},{2,6},{6,2},{3,7},{7,3}} | collective-permute-start | bytes 3538952 | tf_op jit(solution)/shard_map/ppermute | solution.py:558
  336.9 121.5 %collective-permute-start.15 = (bf16[256,2304]{1,0:T(8,128)(2,1)}, bf16[256,2304]{1,0:T(8,128)(2,1)}, u32[]{:S(2)}, u32[]{:S(2)}) collective-permute-start(bf16[256,2304]{1,0:T(8,128)(2,1)} %shard_map.151.refs_12_.refs_1_), channel_id=1, source_target_pairs={{0,4},{4,0},{1,5},{5,1},{2,6},{6,2},{3,7},{7,3}} | collective-permute-start | bytes 3538952 | tf_op jit(solution)/shard_map/ppermute | solution.py:558
  420.2 76.7 %collective-permute-start.23 = (bf16[512,1024]{1,0:T(8,128)(2,1)}, bf16[512,1024]{1,0:T(8,128)(2,1)}, u32[]{:S(2)}, u32[]{:S(2)}) collective-permute-start(bf16[512,1024]{1,0:T(8,128)(2,1)} %get-tuple-element.101.refs_4_), channel_id=1, source_target_pairs={{0,2},{2,0},{1,3},{3,1},{4,6},{6,4},{5,7},{7,5}} | collective-permute-start | bytes 3145736 | tf_op jit(solution)/shard_map/ppermute | solution.py:558
  425.6 58.0 %collective-permute-start.14 = (bf16[256,2304]{1,0:T(8,128)(2,1)}, bf16[256,2304]{1,0:T(8,128)(2,1)}, u32[]{:S(2)}, u32[]{:S(2)}) collective-permute-start(bf16[256,2304]{1,0:T(8,128)(2,1)} %shard_map.153.refs_12_.refs_1_), channel_id=1, source_target_pairs={{0,4},{4,0},{1,5},{5,1},{2,6},{6,2},{3,7},{7,3}} | collective-permute-start | bytes 3538952 | tf_op jit(solution)/shard_map/ppermute | solution.py:558
  445.5 53.1 %collective-permute-start.24 = (bf16[512,1024]{1,0:T(8,128)(2,1)}, bf16[512,1024]{1,0:T(8,128)(2,1)}, u32[]{:S(2)}, u32[]{:S(2)}) collective-permute-start(bf16[512,1024]{1,0:T(8,128)(2,1)} %get-tuple-element.102.refs_5_), channel_id=1, source_target_pairs={{0,2},{2,0},{1,3},{3,1},{4,6},{6,4},{5,7},{7,5}} | collective-permute-start | bytes 3145736 | tf_op jit(solution)/shard_map/ppermute | solution.py:558
  524.5 70.6 %collective-permute-start.31 = (bf16[256,2304]{1,0:T(8,128)(2,1)}, bf16[256,2304]{1,0:T(8,128)(2,1)}, u32[]{:S(2)}, u32[]{:S(2)}) collective-permute-start(bf16[256,2304]{1,0:T(8,128)(2,1)} %collective-permute-done.30.refs_4_), channel_id=1, source_target_pairs={{0,2},{2,0},{1,3},{3,1},{4,6},{6,4},{5,7},{7,5}} | collective-permute-start | bytes 3538952 | tf_op jit(solution)/shard_map/ppermute | solution.py:558
  596.9 100.9 %collective-permute-start.29 = (bf16[512,1024]{1,0:T(8,128)(2,1)}, bf16[512,1024]{1,0:T(8,128)(2,1)}, u32[]{:S(2)}, u32[]{:S(2)}) collective-permute-start(bf16[512,1024]{1,0:T(8,128)(2,1)} %shard_map.158.refs_13_.refs_1_), channel_id=1, source_target_pairs={{0,4},{4,0},{1,5},{5,1},{2,6},{6,2},{3,7},{7,3}} | collective-permute-start | bytes 3145736 | tf_op jit(solution)/shard_map/ppermute | solution.py:558
  696.3 81.8 %collective-permute-start.37 = (bf16[512,1024]{1,0:T(8,128)(2,1)}, bf16[512,1024]{1,0:T(8,128)(2,1)}, u32[]{:S(2)}, u32[]{:S(2)}) collective-permute-start(bf16[512,1024]{1,0:T(8,128)(2,1)} %shard_map.160.refs_13_.refs_1_), channel_id=1, source_target_pairs={{0,4},{4,0},{1,5},{5,1},{2,6},{6,2},{3,7},{7,3}} | collective-permute-start | bytes 3145736 | tf_op jit(solution)/shard_map/ppermute | solution.py:558
  697.5 131.0 %collective-permute-start.36 = (f32[256,2304]{1,0:T(8,128)}, f32[256,2304]{1,0:T(8,128)}, u32[]{:S(2)}, u32[]{:S(2)}) collective-permute-start(f32[256,2304]{1,0:T(8,128)} %get-tuple-element.116), channel_id=1, source_target_pairs={{0,4},{4,0},{1,5},{5,1},{2,6},{6,2},{3,7},{7,3}} | collective-permute-start | bytes 7077896 | tf_op jit(solution)/shard_map/ppermute | solution.py:558
  776.6 56.7 %collective-permute-start.35 = (bf16[512,1024]{1,0:T(8,128)(2,1)}, bf16[512,1024]{1,0:T(8,128)(2,1)}, u32[]{:S(2)}, u32[]{:S(2)}) collective-permute-start(bf16[512,1024]{1,0:T(8,128)(2,1)} %shard_map.162.refs_13_.refs_1_), channel_id=1, source_target_pairs={{0,4},{4,0},{1,5},{5,1},{2,6},{6,2},{3,7},{7,3}} | collective-permute-start | bytes 3145736 | tf_op jit(solution)/shard_map/ppermute | solution.py:558
  777.9 106.5 %collective-permute-start.39 = (f32[256,2304]{1,0:T(8,128)}, f32[256,2304]{1,0:T(8,128)}, u32[]{:S(2)}, u32[]{:S(2)}) collective-permute-start(f32[256,2304]{1,0:T(8,128)} %get-tuple-element.123), channel_id=1, source_target_pairs={{0,4},{4,0},{1,5},{5,1},{2,6},{6,2},{3,7},{7,3}} | collective-permute-start | bytes 7077896 | tf_op jit(solution)/shard_map/ppermute | solution.py:558
  827.3 76.0 %collective-permute-start.42 = (f32[256,2304]{1,0:T(8,128)}, f32[256,2304]{1,0:T(8,128)}, u32[]{:S(2)}, u32[]{:S(2)}) collective-permute-start(f32[256,2304]{1,0:T(8,128)} %get-tuple-element.125), channel_id=1, source_target_pairs={{0,4},{4,0},{1,5},{5,1},{2,6},{6,2},{3,7},{7,3}} | collective-permute-start | bytes 7077896 | tf_op jit(solution)/shard_map/ppermute | solution.py:558
  882.8 124.7 %collective-permute-start.38 = (f32[256,2304]{1,0:T(8,128)}, f32[256,2304]{1,0:T(8,128)}, u32[]{:S(2)}, u32[]{:S(2)}) collective-permute-start(f32[256,2304]{1,0:T(8,128)} %get-tuple-element.121), channel_id=1, source_target_pairs={{0,4},{4,0},{1,5},{5,1},{2,6},{6,2},{3,7},{7,3}} | collective-permute-start | bytes 7077896 | tf_op jit(solution)/shard_map/ppermute | solution.py:558
  883.1 96.0 %collective-permute-start.41 = (bf16[256,2304]{1,0:T(8,128)(2,1)}, bf16[256,2304]{1,0:T(8,128)(2,1)}, u32[]{:S(2)}, u32[]{:S(2)}) collective-permute-start(bf16[256,2304]{1,0:T(8,128)(2,1)} %shard_map.164.refs_13_.refs_1_), channel_id=1, source_target_pairs={{0,4},{4,0},{1,5},{5,1},{2,6},{6,2},{3,7},{7,3}} | collective-permute-start | bytes 3538952 | tf_op jit(solution)/shard_map/ppermute | solution.py:558
  889.0 115.4 %collective-permute-start.40 = (bf16[256,2304]{1,0:T(8,128)(2,1)}, bf16[256,2304]{1,0:T(8,128)(2,1)}, u32[]{:S(2)}, u32[]{:S(2)}) collective-permute-start(bf16[256,2304]{1,0:T(8,128)(2,1)} %shard_map.166.refs_4_.refs_1_), channel_id=1, source_target_pairs={{0,4},{4,0},{1,5},{5,1},{2,6},{6,2},{3,7},{7,3}} | collective-permute-start | bytes 3538952 | tf_op jit(solution)/shard_map/ppermute | solution.py:558
  908.0 121.7 %collective-permute-start.44 = (bf16[256,2304]{1,0:T(8,128)(2,1)}, bf16[256,2304]{1,0:T(8,128)(2,1)}, u32[]{:S(2)}, u32[]{:S(2)}) collective-permute-start(bf16[256,2304]{1,0:T(8,128)(2,1)} %shard_map.167.refs_3_.refs_1_), channel_id=1, source_target_pairs={{0,4},{4,0},{1,5},{5,1},{2,6},{6,2},{3,7},{7,3}} | collective-permute-start | bytes 3538952 | tf_op jit(solution)/shard_map/ppermute | solution.py:558
  (29 other events, 515.4 us)
